TPU v7x, 256 devices: a whole 4x4x8 slice. The times are simulated.
256 devices in a mesh: streams: 16 (over z_lo, x), tm: 16 (over z_hi, y, core).
Axes of the slice: x: 4, y: 4, z: 8 (z_hi: 2, z_lo: 4; z = z_hi * 4 + z_lo), core: 2. Of those that a mesh axis runs over, the one named last changes fastest.
Arguments:
- signal: float32 [2, 16777216], P(None, ('streams', 'tm')), parts along dimension 1, may hold values from -6 to 6
- coarse_taps: float32 [16, 64], replicated, may hold values from -1.5 to 1.5
- fine_taps: float32 [12, 512], replicated, may hold values from -1.8 to 1.8
Outputs:
- channelized: float32 [2, 64, 512, 512], P(None, 'tm', 'streams'), parts along dimension 2
There are 16 independent parts, one for each index of `streams`. A program takes and returns all parts, laid end to end along the dimension named above; an argument that names none is the same for every part. Nothing has to cross between parts.
All inputs are finite; a program needn't handle non-finite values.
Results may differ from a plain program's by a relative error of at most 0.00007.
Values sent between devices are 32-bit elements; how exact they have to be, the bound alone decides.
A program may use at most 320 MiB of HBM per device.

v0:
```python
import math

import jax
import jax.numpy as jnp
from jax import lax
from jax.sharding import Mesh
from jax.sharding import PartitionSpec as P

CHANNELS = 64
FINE = 512
TAPS = 16
FINE_TAPS = 12
TM = ("tm_0", "tm_1", "tm_2")
STREAMS_TM = ("streams", "tm_0", "tm_1", "tm_2")


def from_behind(array, axis, by):
    length = lax.axis_size(axis)
    pairs = [(i, i + by) for i in range(length) if 0 <= i + by < length]
    return lax.ppermute(array, axis, pairs)


def split_up(array, dim, length):
    shape = array.shape
    blocks = array.reshape(*shape[:dim], length, shape[dim] // length, *shape[dim + 1 :])
    return jnp.moveaxis(blocks, dim, 0)


def laid_out(blocks, dim):
    shape = list(blocks.shape[1:])
    shape[dim] *= blocks.shape[0]
    return jnp.moveaxis(blocks, 0, dim).reshape(shape)


def turned_blocks(blocks, axes, turns):
    shape = [lax.axis_size(a) for a in axes]
    blocks = blocks.reshape(*shape, *blocks.shape[1:])
    for k in turns:
        blocks = lax.all_to_all(blocks, axes[k], split_axis=k, concat_axis=k, tiled=True)
    return blocks.reshape(-1, *blocks.shape[len(axes) :])


def two_step_exchange(array, groups, turns, split_dim, concat_dim):
    length = lax.axis_size(groups[0]) * lax.axis_size(groups[1])
    blocks = split_up(array, split_dim, length)
    return laid_out(turned_blocks(blocks, groups, turns), concat_dim)


def tables(points):
    counter = jnp.arange(points, dtype=jnp.int32)
    product = counter[:, None] * counter[None, :] % points
    angle = product.astype(jnp.float32) * (2.0 * math.pi / points)
    return (jnp.cos(angle), jnp.sin(angle))


def coarse_branches(extended, coarse_taps, length):
    row_count = length // (2 * CHANNELS)
    summed = jnp.zeros((2, row_count, 2 * CHANNELS), jnp.float32)
    for tap_index in range(TAPS):
        offset = (TAPS - 1 - tap_index) * CHANNELS
        segment = extended[:, offset : offset + length].reshape(2, row_count, 2 * CHANNELS)
        summed = summed + segment * jnp.tile(coarse_taps[tap_index], 2)
    return summed.reshape(2, length // CHANNELS, CHANNELS)


def coarse_spectrum(branches, cosine_rows, sine_rows):
    factor = 1.0 / math.sqrt(CHANNELS)
    highest = lax.Precision.HIGHEST
    real_part = (
        jnp.einsum("kp,tp->kt", cosine_rows, branches[0], precision=highest)
        + jnp.einsum("kp,tp->kt", sine_rows, branches[1], precision=highest)
    ) * factor
    imag_part = (
        jnp.einsum("kp,tp->kt", cosine_rows, branches[1], precision=highest)
        - jnp.einsum("kp,tp->kt", sine_rows, branches[0], precision=highest)
    ) * factor
    return jnp.stack([real_part, imag_part])


def fine_section(coarse, fine_taps):
    group_size = coarse.shape[1]
    fine_frames = coarse.shape[2] // FINE
    shaped = coarse.reshape(2, group_size, fine_frames, FINE)
    padded = jnp.pad(shaped, ((0, 0), (0, 0), (FINE_TAPS - 1, 0), (0, 0)))
    summed = jnp.zeros((2, group_size, fine_frames, FINE), jnp.float32)
    for tap_index in range(FINE_TAPS):
        offset = FINE_TAPS - 1 - tap_index
        summed = summed + fine_taps[tap_index] * padded[:, :, offset : offset + fine_frames, :]
    cosine_table, sine_table = tables(FINE)
    factor = 1.0 / math.sqrt(FINE)
    highest = lax.Precision.HIGHEST
    out_real = (
        jnp.matmul(summed[0], cosine_table, precision=highest)
        + jnp.matmul(summed[1], sine_table, precision=highest)
    ) * factor
    out_imag = (
        jnp.matmul(summed[1], cosine_table, precision=highest)
        - jnp.matmul(summed[0], sine_table, precision=highest)
    ) * factor
    return jnp.stack([out_real, out_imag])


def on_device(signal, coarse_taps, fine_taps):
    length = signal.shape[1]
    history = (TAPS - 1) * CHANNELS
    cosine_table, sine_table = tables(CHANNELS)
    previous = from_behind(signal[:, length - history :], TM, 1)
    extended = jnp.concatenate([previous, signal], axis=1)
    branches = coarse_branches(extended, coarse_taps, length)
    coarse = two_step_exchange(
        coarse_spectrum(branches, cosine_table, sine_table),
        (("tm_0", "tm_1"), "tm_2"),
        (0, 1),
        1,
        2,
    )
    return fine_section(coarse, fine_taps)


def solution(mesh):
    finer = Mesh(
        mesh.devices.reshape(mesh.shape["streams"], 2, 4, 2), ("streams", "tm_0", "tm_1", "tm_2")
    )
    placed = (P(None, STREAMS_TM), P(), P())
    return jax.shard_map(
        on_device,
        mesh=finer,
        in_specs=placed,
        out_specs=P(None, TM, "streams", None),
        check_vma=False,
    )
```

profile of v0, /device:TPU:32, one launch (start us, length us, event | category | flops | bytes accessed | tf_op | source)
XLA Modules:
  0.0 74.7 jit_solution(10461954945009727881)
XLA Ops:
  0.0 0.8 %slice.186 = f32[2,960]{1,0:T(2,128)S(1)} slice(f32[2,65536]{1,0:T(2,128)} %param.3), slice={[0:2], [64576:65536]} | slice | bytes 15360 | tf_op jit(solution)/shard_map/slice | solution.py:107
  0.8 1.7 %collective-permute-start = (f32[2,960]{1,0:T(2,128)S(1)}, f32[2,960]{1,0:T(2,128)S(1)}, u32[]{:S(2)}, u32[]{:S(2)}) collective-permute-start(f32[2,960]{1,0:T(2,128)S(1)} %slice.186), channel_id=1, source_target_pairs={{0,1},{1,2},{2,3},{3,4},{4,5},{5,6},{6,7},{7,8},{8,9},{9,10},{10,1... | collective-permute-start | bytes 23048 | tf_op jit(solution)/shard_map/ppermute | solution.py:20
  4.0 4.7 %fusion.43 = (f32[1,2,512,128]{3,1,2,0:T(2,128)S(1)}, f32[1,2,512,128]{3,1,2,0:T(2,128)S(1)}, f32[1,2,512,128]{3,1,2,0:T(2,128)S(1)}, f32[1,2,512,128]{3,1,2,0:T...) fusion(f32[2,960]{1,0:T(2,128)S(1)} %collective-permute-done, f32[2,65536]{1,0:T(2,128)} %param.3), kind=kLoop, calls=%fused_computation.75 | loop fusion | flops 786432 | bytes 3677696
  8.6 2.6 %fusion.55 = (f32[1,2,512,128]{3,1,2,0:T(2,128)S(1)}, f32[1,2,512,128]{3,1,2,0:T(2,128)S(1)}, f32[1,2,512,128]{3,1,2,0:T(2,128)S(1)}, f32[1,2,512,128]{3,1,2,0:T...) fusion(f32[2,960]{1,0:T(2,128)S(1)} %collective-permute-done, f32[2,65536]{1,0:T(2,128)S(1)} %copy-done), kind=kLoop, calls=%fused_computation.87 | loop fusion | flops 786432 | bytes 3677696
  11.2 1.3 %fusion.67 = (f32[1,2,512,128]{3,1,2,0:T(2,128)S(1)}, f32[1,2,512,128]{3,1,2,0:T(2,128)S(1)}, f32[1,2,512,128]{3,1,2,0:T(2,128)S(1)}) fusion(f32[2,960]{1,0:T(2,128)S(1)} %collective-permute-done, f32[2,65536]{1,0:T(2,128)S(1)} %copy-done), kind=kLoop, calls=%fused_computation.99 | loop fusion | flops 393216 | bytes 2104832
  12.5 0.6 fusion.68
  13.1 0.1 squeeze.16
  13.3 0.8 %fusion.100 = f32[64,1024]{1,0:T(8,128)S(1)} fusion(f32[1024,64]{1,0:T(8,128)S(1)} %squeeze.16), kind=kOutput, calls=%fused_computation.151 | convolution fusion | flops 50388992 | bytes 524288 | tf_op jit(solution)/shard_map/kp,tp->kt/dot_general | solution.py:70
  14.1 0.2 squeeze.17
  14.3 0.8 %fusion.98 = f32[64,1024]{1,0:T(8,128)S(1)} fusion(f32[1024,64]{1,0:T(8,128)S(1)} %squeeze.17), kind=kOutput, calls=%fused_computation.150 | convolution fusion | flops 50388992 | bytes 524288 | tf_op jit(solution)/shard_map/kp,tp->kt/dot_general | solution.py:74
  15.1 0.8 %fusion.1 = f32[64,1024]{1,0:T(8,128)S(1)} fusion(f32[64,1024]{1,0:T(8,128)S(1)} %fusion.100, f32[1024,64]{1,0:T(8,128)S(1)} %squeeze.17), kind=kOutput, calls=%fused_computation.31 | convolution fusion | flops 50520064 | bytes 786432 | tf_op jit(solution)/shard_map/kp,tp->kt/dot_general | solution.py:71
  16.0 0.8 %fusion = f32[64,1024]{1,0:T(8,128)S(1)} fusion(f32[64,1024]{1,0:T(8,128)S(1)} %fusion.98, f32[1024,64]{1,0:T(8,128)S(1)} %squeeze.16), kind=kOutput, calls=%fused_computation.29 | convolution fusion | flops 50520064 | bytes 786432 | tf_op jit(solution)/shard_map/kp,tp->kt/dot_general | solution.py:75
  16.9 0.1 pad_maximum_fusion.1
  17.0 0.8 %copy.9 = f32[8,2,2,4,1024]{4,3,1,2,0:T(4,128)} copy(f32[8,2,2,4,1024]{4,3,2,1,0:T(4,128)S(1)} %bitcast.204) | data formatting | bytes 1048576 | tf_op jit(solution)/shard_map/reshape | solution.py:37
  17.8 15.5 %all-to-all-start = ((f32[8,2,2,4,1024]{4,3,1,2,0:T(4,128)}), f32[8,2,2,4,1024]{4,3,1,2,0:T(4,128)S(1)}, u32[]{:S(2)}, u32[]{:S(2)}) async-start(f32[8,2,2,4,1024]{4,3,1,2,0:T(4,128)} %copy.9), calls=%async_computation | async-start | bytes 1048576 | tf_op jit(solution)/shard_map/all_to_all | solution.py:39
  33.4 15.8 %all-to-all-done = f32[8,2,2,4,1024]{4,3,1,2,0:T(4,128)S(1)} async-done(((f32[8,2,2,4,1024]{4,3,1,2,0:T(4,128)}), f32[8,2,2,4,1024]{4,3,1,2,0:T(4,128)S(1)}, u32[]{:S(2)}, u32[]{:S(2)}) %all-to-all-start) | async-done | bytes 524320 | tf_op jit(solution)/shard_map/all_to_all | solution.py:39
  49.1 4.2 %all_to_all.10 = f32[8,2,2,4,1024]{4,3,0,2,1:T(4,128)S(1)} all-to-all(f32[8,2,2,4,1024]{4,3,0,2,1:T(4,128)S(1)} %copy.10), channel_id=1, replica_groups=mesh['streams'=16,'tm_0'=2,'tm_1'=4,'tm_2'=2] {'tm_2'}, dimensions={1} | all-to-all | bytes 1048576 | tf_op jit(solution)/shard_map/all_to_all | solution.py:39
  53.3 0.3 copy.12
  53.7 0.7 fusion.29
  54.4 4.9 %fusion.13 = f32[4,32,512]{2,1,0:T(8,128)S(1)} fusion(f32[2,4,32,512]{3,2,1,0:T(8,128)S(1)} %fusion.29), kind=kOutput, calls=%fused_computation.45 | convolution fusion | flops 406323200 | bytes 524288 | tf_op jit(solution)/shard_map/dot_general | solution.py:93
  59.3 4.9 %fusion.11 = f32[4,32,512]{2,1,0:T(8,128)S(1)} fusion(f32[2,4,32,512]{3,2,1,0:T(8,128)S(1)} %fusion.29), kind=kOutput, calls=%fused_computation.43 | convolution fusion | flops 406323200 | bytes 524288 | tf_op jit(solution)/shard_map/dot_general | solution.py:97
  64.1 4.8 %fusion.5 = f32[1,4,32,512]{3,2,1,0:T(8,128)S(1)} fusion(f32[4,32,512]{2,1,0:T(8,128)S(1)} %fusion.13, f32[2,4,32,512]{3,2,1,0:T(8,128)S(1)} %fusion.29), kind=kOutput, calls=%fused_computation.37 | convolution fusion | flops 406454272 | bytes 786432 | tf_op jit(solution)/shard_map/dot_general | solution.py:94
  69.0 4.8 %fusion.3 = f32[1,4,32,512]{3,2,1,0:T(8,128)S(1)} fusion(f32[4,32,512]{2,1,0:T(8,128)S(1)} %fusion.11, f32[2,4,32,512]{3,2,1,0:T(8,128)S(1)} %fusion.29), kind=kOutput, calls=%fused_computation.34 | convolution fusion | flops 406454272 | bytes 786432 | tf_op jit(solution)/shard_map/dot_general | solution.py:98
  73.9 0.8 %pad_maximum_fusion.2 = f32[2,4,32,512]{3,2,1,0:T(8,128)} fusion(f32[1,4,32,512]{3,2,1,0:T(8,128)S(1)} %fusion.3, f32[1,4,32,512]{3,2,1,0:T(8,128)S(1)} %fusion.5), kind=kLoop, calls=%fused_computation.134 | loop fusion | flops 131072 | bytes 1048576 | tf_op jit(solution)/shard_map/stack | solution.py:100
  (47 shorter events, 1.8 us)
Async XLA Ops:
  0.0 2.5 %copy-start.2 = (f32[16,64]{1,0:T(8,128)S(1)}, f32[16,64]{1,0:T(8,128)}, u32[]{:S(2)}) copy-start(f32[16,64]{1,0:T(8,128)} %param.4) | copy-start | bytes 12292
  0.8 3.2 %collective-permute-start = (f32[2,960]{1,0:T(2,128)S(1)}, f32[2,960]{1,0:T(2,128)S(1)}, u32[]{:S(2)}, u32[]{:S(2)}) collective-permute-start(f32[2,960]{1,0:T(2,128)S(1)} %slice.186), channel_id=1, source_target_pairs={{0,1},{1,2},{2,3},{3,4},{4,5},{5,6},{6,7},{7,8},{8,9},{9,10},{10,1... | collective-permute-start | bytes 23048 | tf_op jit(solution)/shard_map/ppermute | solution.py:20
  4.0 4.7 %copy-start = (f32[2,65536]{1,0:T(2,128)S(1)}, f32[2,65536]{1,0:T(2,128)}, u32[]{:S(2)}) copy-start(f32[2,65536]{1,0:T(2,128)} %param.3) | copy-start | bytes 1572868
  17.8 15.5 %copy-start.1 = (f32[12,512]{1,0:T(8,128)S(1)}, f32[12,512]{1,0:T(8,128)}, u32[]{:S(2)}) copy-start(f32[12,512]{1,0:T(8,128)} %param.5) | copy-start | bytes 73732
  17.8 31.3 %all-to-all-start = ((f32[8,2,2,4,1024]{4,3,1,2,0:T(4,128)}), f32[8,2,2,4,1024]{4,3,1,2,0:T(4,128)S(1)}, u32[]{:S(2)}, u32[]{:S(2)}) async-start(f32[8,2,2,4,1024]{4,3,1,2,0:T(4,128)} %copy.9), calls=%async_computation | async-start | bytes 1048576 | tf_op jit(solution)/shard_map/all_to_all | solution.py:39
where the time goes:
time: 75.4 us; the launch traced here: 74.7 us
  matrix products  22.6 us (30%)
  starting transfers between devices  17.2 us (23%)
  waiting for transfers between devices  15.8 us (21%)
  other arithmetic  10.7 us (14%)
  blocking collectives  4.15 us (6%)
  local copies, waits for them, and re-layouts  3.98 us (5%)
    all_to_all x1, waiting for transfers between devices, turned_blocks(): lax.all_to_all(blocks, axes[k], split_axis=k, concat_axis=k, tiled=True)  15.8 us
    all_to_all x1, starting transfers between devices, turned_blocks(): lax.all_to_all(blocks, axes[k], split_axis=k, concat_axis=k, tiled=True)  15.5 us
    unnamed x3, other arithmetic  8.52 us
    dot_general x1, matrix products, fine_section(): jnp.matmul(summed[0], cosine_table, precision=highest)  4.86 us
    dot_general x1, matrix products, fine_section(): jnp.matmul(summed[1], cosine_table, precision=highest)  4.86 us
    dot_general x1, matrix products, fine_section(): jnp.matmul(summed[1], sine_table, precision=highest)  4.85 us
    dot_general x1, matrix products, fine_section(): jnp.matmul(summed[0], sine_table, precision=highest)  4.85 us
    all_to_all x1, blocking collectives, turned_blocks(): lax.all_to_all(blocks, axes[k], split_axis=k, concat_axis=k, tiled=True)  4.15 us
  transfers between devices with their start and end apart: 2, of which 1 were waited for; matrix products, arithmetic and copies ran while one was open for 2% of the time, Pallas kernels for 0%

commit v1 on v0

v1 whole, which is shorter than its diff:
```python
import functools
import math

import jax
import jax.numpy as jnp
import numpy as np
from jax import lax
from jax.experimental import pallas as pl
from jax.experimental.pallas import tpu as pltpu
from jax.sharding import Mesh
from jax.sharding import PartitionSpec as P

CHANNELS = 64
FINE = 512
TAPS = 16
FINE_TAPS = 12
TM = ("zh", "y", "c")
GROUP = (2, 4, 2)
PEERS = 16
LANES = 128
HALO = 16
ROWS = 1024
HALF = 512
MESH = pl.DeviceIdType.MESH
OTHERS = [
    (dz, dy, dc)
    for dz in (1, 0)
    for dy in (2, 1, 3, 0)
    for dc in (1, 0)
    if (dz, dy, dc) != (0, 0, 0)
]


def split(value):
    high = value.astype(jnp.bfloat16)
    low = (value - high.astype(jnp.float32)).astype(jnp.bfloat16)
    return high, low


def np_split(value):
    value = value.astype(np.float32)
    high = value.astype(jnp.bfloat16)
    low = (value - high.astype(np.float32)).astype(jnp.bfloat16)
    return high, low


def coarse_matrix():
    owner, part, own, parity = np.meshgrid(
        np.arange(16), np.arange(2), np.arange(4), np.arange(2), indexing="ij"
    )
    channel = (4 * owner + own).reshape(-1, 1)
    part, parity = part.reshape(-1, 1), parity.reshape(-1, 1)
    part_in, parity_in, branch = np.meshgrid(
        np.arange(2), np.arange(2), np.arange(CHANNELS), indexing="ij"
    )
    part_in, parity_in, branch = (v.reshape(1, -1) for v in (part_in, parity_in, branch))
    angle = 2.0 * np.pi * (channel * branch % CHANNELS) / CHANNELS
    value = np.where(part == part_in, np.cos(angle), np.sin(angle) * (part_in - part))
    value = np.where(parity == parity_in, value, 0.0) / math.sqrt(CHANNELS)
    high, low = np_split(value)
    return np.concatenate([high, low, high], axis=1)


def fine_matrix():
    part_in, b = np.meshgrid(np.arange(2), np.arange(LANES), indexing="ij")
    part_in, b = part_in.reshape(-1, 1), b.reshape(-1, 1)
    part, c = part_in.reshape(1, -1), b.reshape(1, -1)
    angle = 2.0 * np.pi * (b * c % LANES) / LANES
    value = np.where(part == part_in, np.cos(angle), np.sin(angle) * (part_in - part))
    high, low = np_split(value / math.sqrt(FINE))
    return np.concatenate([high, low, high], axis=0)


def twiddles():
    a, c = np.meshgrid(np.arange(4), np.arange(LANES), indexing="ij")
    angle = 2.0 * np.pi * a * c / FINE
    return np.concatenate([np.cos(angle), np.sin(angle)]).astype(np.float32)


def place():
    return tuple(lax.axis_index(a) for a in TM)


def shifted(me, by):
    return tuple(lax.rem(m + d, n) for m, d, n in zip(me, by, GROUP, strict=True))


def flat(at):
    return (at[0] * 4 + at[1]) * 2 + at[2]


def named(at):
    return dict(zip(TM, at, strict=True))


def gather_kernel(
    x_hbm, m_hbm, ct_hbm, ft_hbm, got, taps_out,
    xs, ys, ms, ct, ft, ftt, sent, load_sem, halo_sem, send_sem, recv_sem,
):
    me = place()
    mine = flat(me)
    barrier = pltpu.get_barrier_semaphore()
    for by in OTHERS:
        pl.semaphore_signal(barrier, inc=1, device_id=named(shifted(me, by)), device_id_type=MESH)
    loads = [
        pltpu.make_async_copy(x_hbm, xs.at[pl.ds(HALO, ROWS)], load_sem.at[0]),
        pltpu.make_async_copy(m_hbm, ms, load_sem.at[1]),
        pltpu.make_async_copy(ct_hbm, ct, load_sem.at[2]),
        pltpu.make_async_copy(ft_hbm, ft, load_sem.at[3]),
    ]
    for load in loads:
        load.start()
    loads[2].wait()
    taps = ct[...]
    taps = jnp.concatenate([taps, taps], axis=1)
    loads[0].wait()
    loads[1].wait()

    def delay(start, size):
        first = lax.broadcasted_iota(jnp.int32, (size, LANES), 1) < CHANNELS
        here = xs[pl.ds(start, size), :]
        before = xs[pl.ds(start - 2, size), :]
        ys[pl.ds(start, size), :] = pltpu.roll(jnp.where(first, here, before), CHANNELS, 1)

    def filtered(m):
        pieces = []
        for a1 in range(2):
            for c in range(2):
                acc = None
                for i in range(TAPS // 2):
                    at = HALO + HALF * m + 2 * a1 + c - 2 * i
                    rows = pl.ds(at, LANES, stride=4)
                    term = taps[2 * i : 2 * i + 1] * xs[rows, :]
                    acc = term if acc is None else acc + term
                    acc = acc + taps[2 * i + 1 : 2 * i + 2] * ys[rows, :]
                pieces.append(acc)
        full = jnp.concatenate(
            [
                jnp.concatenate(pieces[0:2], axis=1),
                jnp.concatenate(pieces[2:4], axis=1),
            ],
            axis=0,
        )
        high, low = split(full)
        right = jnp.concatenate([high, high, low], axis=1)
        result = lax.dot_general(
            ms[...], right, (((1,), (1,)), ((), ())), preferred_element_type=jnp.float32
        )
        sent[m] = result.reshape(PEERS, 16, 256)
        got[m, mine] = sent[m, mine]

    def send(m):
        copies = []
        for k, by in enumerate(OTHERS):
            to = shifted(me, by)
            copy = pltpu.make_async_remote_copy(
                src_ref=sent.at[m, flat(to)],
                dst_ref=got.at[m, mine],
                send_sem=send_sem.at[m, k],
                recv_sem=recv_sem.at[m, k],
                device_id=named(to),
                device_id_type=MESH,
            )
            copy.start()
            copies.append(copy)
        return copies

    delay(HALO + HALF - 16, HALF + 16)
    filtered(1)
    pl.semaphore_wait(barrier, len(OTHERS))
    last = mine == PEERS - 1
    after = lax.rem(mine + 1, PEERS)
    halo = pltpu.make_async_remote_copy(
        src_ref=xs.at[pl.ds(ROWS, HALO)],
        dst_ref=xs.at[pl.ds(0, HALO)],
        send_sem=halo_sem.at[0],
        recv_sem=halo_sem.at[1],
        device_id=named((after // 8, lax.rem(after // 2, 4), lax.rem(after, 2))),
        device_id_type=MESH,
    )

    @pl.when(jnp.logical_not(last))
    def _():
        halo.start()

    copies = send(1)

    @pl.when(mine == 0)
    def _():
        xs[pl.ds(0, HALO), :] = jnp.zeros((HALO, LANES), jnp.float32)

    @pl.when(mine > 0)
    def _():
        halo.wait_recv()

    delay(2, HALF + HALO - 16 - 2)
    filtered(0)
    copies += send(0)

    loads[3].wait()
    square = jnp.concatenate([ft[...], jnp.zeros((LANES - FINE_TAPS, FINE), jnp.float32)], axis=0)
    for k in range(4):
        ftt[pl.ds(LANES * k, LANES), :] = square[:, LANES * k : LANES * (k + 1)].T
    by_branch = [ftt[pl.ds(a, LANES, stride=4), :].T for a in range(4)]
    odd = lax.rem(lax.broadcasted_iota(jnp.int32, (8, LANES), 0), 2) == 1
    for a1 in range(2):
        for j in range(FINE_TAPS):
            even_row = jnp.broadcast_to(by_branch[2 * a1][j : j + 1], (8, LANES))
            odd_row = jnp.broadcast_to(by_branch[2 * a1 + 1][j : j + 1], (8, LANES))
            taps_out[a1, j] = jnp.where(odd, odd_row, even_row)

    for copy in copies:
        copy.wait()

    @pl.when(jnp.logical_not(last))
    def _():
        halo.wait_send()


def fine_kernel(got, taps, cm, tw, out, fir, stage, out_sem):
    for a1 in range(2):
        for c in range(2):
            for frame in range(32):
                acc = None
                for j in range(min(FINE_TAPS, frame + 1)):
                    at = frame - j
                    block = got[at % 2, at // 2, pl.ds(8 * c, 8), pl.ds(LANES * a1, LANES)]
                    term = taps[a1, j] * block
                    acc = term if acc is None else acc + term
                fir[a1, c, pl.ds(8 * frame, 8), :] = acc
    cosine = tw[pl.ds(0, 4), :]
    sine = tw[pl.ds(4, 4), :]
    writes = []
    for k in range(4):
        rows = []
        for a in range(4):
            parts = [fir[a // 2, c, pl.ds(2 * k + a % 2, 32, stride=8), :] for c in range(2)]
            rows.append(jnp.concatenate(parts, axis=1))
        left = jnp.concatenate(rows, axis=0)
        high, low = split(left)
        left = jnp.concatenate([high, high, low], axis=1)
        spectrum = jnp.dot(left, cm[...], preferred_element_type=jnp.float32)
        real, imag = [], []
        for a in range(4):
            re = spectrum[32 * a : 32 * a + 32, :LANES]
            im = spectrum[32 * a : 32 * a + 32, LANES:]
            if a:
                cos, sin = cosine[a : a + 1], sine[a : a + 1]
                re, im = re * cos + im * sin, im * cos - re * sin
            real.append(re)
            imag.append(im)
        sum_re, sum_im = real[0] + real[2], imag[0] + imag[2]
        dif_re, dif_im = real[0] - real[2], imag[0] - imag[2]
        odd_re, odd_im = real[1] + real[3], imag[1] + imag[3]
        off_re, off_im = real[1] - real[3], imag[1] - imag[3]
        stage[k, 0, :, 0:128] = sum_re + odd_re
        stage[k, 1, :, 0:128] = sum_im + odd_im
        stage[k, 0, :, 128:256] = dif_re + off_im
        stage[k, 1, :, 128:256] = dif_im - off_re
        stage[k, 0, :, 256:384] = sum_re - odd_re
        stage[k, 1, :, 256:384] = sum_im - odd_im
        stage[k, 0, :, 384:512] = dif_re - off_im
        stage[k, 1, :, 384:512] = dif_im + off_re
        for c in range(2):
            write = pltpu.make_async_copy(stage.at[k, c], out.at[c, k], out_sem.at[k, c])
            write.start()
            writes.append(write)
    for write in writes:
        write.wait()


def on_device(signal, coarse_taps, fine_taps):
    rows = signal.reshape(2, HALF, LANES).transpose(1, 0, 2).reshape(ROWS, LANES)
    anywhere = pl.BlockSpec(memory_space=pl.ANY)
    vmem = pl.BlockSpec(memory_space=pltpu.VMEM)
    got, taps = pl.pallas_call(
        gather_kernel,
        out_shape=[
            jax.ShapeDtypeStruct((2, PEERS, 16, 256), jnp.float32),
            jax.ShapeDtypeStruct((2, FINE_TAPS, 8, LANES), jnp.float32),
        ],
        in_specs=[anywhere] * 4,
        out_specs=[vmem, vmem],
        scratch_shapes=[
            pltpu.VMEM((HALO + ROWS, LANES), jnp.float32),
            pltpu.VMEM((HALO + ROWS, LANES), jnp.float32),
            pltpu.VMEM((256, 768), jnp.bfloat16),
            pltpu.VMEM((TAPS, CHANNELS), jnp.float32),
            pltpu.VMEM((FINE_TAPS, FINE), jnp.float32),
            pltpu.VMEM((FINE, LANES), jnp.float32),
            pltpu.VMEM((2, PEERS, 16, 256), jnp.float32),
            pltpu.SemaphoreType.DMA((4,)),
            pltpu.SemaphoreType.DMA((2,)),
            pltpu.SemaphoreType.DMA((2, len(OTHERS))),
            pltpu.SemaphoreType.DMA((2, len(OTHERS))),
        ],
        compiler_params=pltpu.CompilerParams(collective_id=0, has_side_effects=True),
        name="gather",
    )(rows, jnp.asarray(coarse_matrix()), coarse_taps, fine_taps)
    return pl.pallas_call(
        fine_kernel,
        out_shape=jax.ShapeDtypeStruct((2, 4, 32, FINE), jnp.float32),
        in_specs=[vmem] * 4,
        out_specs=anywhere,
        scratch_shapes=[
            pltpu.VMEM((2, 2, 256, LANES), jnp.float32),
            pltpu.VMEM((4, 2, 32, FINE), jnp.float32),
            pltpu.SemaphoreType.DMA((4, 2)),
        ],
        name="fine",
    )(got, taps, jnp.asarray(fine_matrix()), jnp.asarray(twiddles()))


def solution(mesh):
    finer = Mesh(mesh.devices.reshape(mesh.shape["streams"], *GROUP), ("streams", *TM))
    return jax.shard_map(
        on_device,
        mesh=finer,
        in_specs=(P(None, ("streams", *TM)), P(), P()),
        out_specs=P(None, TM, "streams", None),
        check_vma=False,
    )
```

time: 75.4 us -> 31.1 us (0.41)
  the two profiles are of different devices: /device:TPU:32 before, /device:TPU:1 now
where the time goes in v1:
time: 31.1 us; the launch traced here: 31 us
  Pallas kernels  31 us (100%)
    pallas_call x1, Pallas kernels, on_device(): pl.pallas_call(gather_kernel, out_shape=[jax.ShapeDtypeStruct((2, PEERS,...  28.2 us
    pallas_call x1, Pallas kernels, on_device(): pl.pallas_call(fine_kernel, out_shape=jax.ShapeDtypeStruct((2, 4, 32, FIN...  2.72 us

profile of v1, /device:TPU:1, one launch (start us, length us, event | category | flops | bytes accessed | tf_op | source)
XLA Modules:
  0.0 31.0 jit_solution(4618670013445334403)
XLA Ops:
  0.0 28.2 %gather.1 = (f32[2,16,16,256]{3,2,1,0:T(8,128)}, f32[2,12,8,128]{3,2,1,0:T(8,128)}) custom-call(f32[1024,128]{1,0:T(8,128)} %bitcast.5, bf16[256,768]{1,0:T(8,128)(2,1)} %constant.6.clone.m_hbm, f32[16,64]{1,0:T(8,128)} %ct_hbm.1, f32[12,512]{1,0:T(8,128)} %ft_hbm.1), custom_call_target="tpu_custom_call" | custom-call | tf_op jit(solution)/shard_map/gather/pallas_call | solution.py:276
  28.3 2.7 %fine.1 = f32[2,4,32,512]{3,2,1,0:T(8,128)} custom-call(f32[2,16,16,256]{3,2,1,0:T(8,128)} %get-tuple-element.7.got, f32[2,12,8,128]{3,2,1,0:T(8,128)} %get-tuple-element.8.taps, bf16[768,256]{1,0:T(8,128)(2,1)} %constant.7.clone.cm, f32[8,128]{1,0:T(8,128)} %constant.8.clone.tw), custom_call_target="tpu_custom_call" | custom-call | tf_op jit(solution)/shard_map/fine/pallas_call | solution.py:300

commit v2 on v1

v2 whole, which is shorter than its diff:
```python
import functools
import math

import jax
import jax.numpy as jnp
import numpy as np
from jax import lax
from jax.experimental import pallas as pl
from jax.experimental.pallas import tpu as pltpu
from jax.sharding import Mesh
from jax.sharding import PartitionSpec as P

CHANNELS = 64
FINE = 512
TAPS = 16
FINE_TAPS = 12
TM = ("zh", "y", "c")
GROUP = (2, 4, 2)
PEERS = 16
LANES = 128
HEAD = 16
TAIL = 32
ROWS = 1024
HALF = 512
MESH = pl.DeviceIdType.MESH
OTHERS = [
    (dz, dy, dc)
    for dz in (1, 0)
    for dy in (2, 1, 3, 0)
    for dc in (1, 0)
    if (dz, dy, dc) != (0, 0, 0)
]


def split(value):
    high = value.astype(jnp.bfloat16)
    low = (value - high.astype(jnp.float32)).astype(jnp.bfloat16)
    return high, low


def np_split(value):
    value = value.astype(np.float32)
    high = value.astype(jnp.bfloat16)
    low = (value - high.astype(np.float32)).astype(jnp.bfloat16)
    return high, low


def coarse_matrix():
    owner, part, own, parity = np.meshgrid(
        np.arange(16), np.arange(2), np.arange(4), np.arange(2), indexing="ij"
    )
    channel = (4 * owner + own).reshape(-1, 1)
    part, parity = part.reshape(-1, 1), parity.reshape(-1, 1)
    part_in, parity_in, branch = np.meshgrid(
        np.arange(2), np.arange(2), np.arange(CHANNELS), indexing="ij"
    )
    part_in, parity_in, branch = (v.reshape(1, -1) for v in (part_in, parity_in, branch))
    angle = 2.0 * np.pi * (channel * branch % CHANNELS) / CHANNELS
    value = np.where(part == part_in, np.cos(angle), np.sin(angle) * (part_in - part))
    value = np.where(parity == parity_in, value, 0.0) / math.sqrt(CHANNELS)
    high, low = np_split(value)
    return np.concatenate([high, low, high], axis=1)


def fine_matrix():
    part_in, b = np.meshgrid(np.arange(2), np.arange(LANES), indexing="ij")
    part_in, b = part_in.reshape(-1, 1), b.reshape(-1, 1)
    part, c = part_in.reshape(1, -1), b.reshape(1, -1)
    angle = 2.0 * np.pi * (b * c % LANES) / LANES
    value = np.where(part == part_in, np.cos(angle), np.sin(angle) * (part_in - part))
    high, low = np_split(value / math.sqrt(FINE))
    return np.concatenate([high, low, high], axis=0)


def twiddles():
    a, c = np.meshgrid(np.arange(4), np.arange(LANES), indexing="ij")
    angle = 2.0 * np.pi * a * c / FINE
    return np.concatenate([np.cos(angle), np.sin(angle)]).astype(np.float32)


def place():
    return tuple(lax.axis_index(a) for a in TM)


def shifted(me, by):
    return tuple(lax.rem(m + d, n) for m, d, n in zip(me, by, GROUP, strict=True))


def flat(at):
    return (at[0] * 4 + at[1]) * 2 + at[2]


def named(at):
    return dict(zip(TM, at, strict=True))


def coarse_frames(xs, ys, taps, start, size):
    parts = []
    for c in range(2):
        acc = None
        for i in range(TAPS // 2):
            rows = pl.ds(HEAD + start + c - 2 * i, size, stride=4)
            term = taps[2 * i : 2 * i + 1] * xs[rows, :]
            acc = term if acc is None else acc + term
            acc = acc + taps[2 * i + 1 : 2 * i + 2] * ys[rows, :]
        parts.append(acc)
    return jnp.concatenate(parts, axis=1)


def spectra(ms, frames):
    high, low = split(frames)
    right = jnp.concatenate([high, high, low], axis=1)
    return lax.dot_general(
        ms[...], right, (((1,), (1,)), ((), ())), preferred_element_type=jnp.float32
    )


def fine_filter(a1, block, taps, fir):
    for c in range(2):
        for frame in range(32):
            acc = None
            for j in range(min(FINE_TAPS, frame + 1)):
                term = taps(j) * block(c, frame - j)
                acc = term if acc is None else acc + term
            fir[c, pl.ds(8 * frame, 8), :] = acc


def fine_spectra(a1, k, fir, cm, tw):
    rows = []
    for h in range(2):
        parts = [fir[c, pl.ds(2 * k + h, 32, stride=8), :] for c in range(2)]
        rows.append(jnp.concatenate(parts, axis=1))
    high, low = split(jnp.concatenate(rows, axis=0))
    left = jnp.concatenate([high, high, low], axis=1)
    spectrum = jnp.dot(left, cm[...], preferred_element_type=jnp.float32)
    result = []
    for h in range(2):
        a = 2 * a1 + h
        re = spectrum[32 * h : 32 * h + 32, :LANES]
        im = spectrum[32 * h : 32 * h + 32, LANES:]
        if a:
            cos, sin = tw[a : a + 1, :], tw[4 + a : 5 + a, :]
            re, im = re * cos + im * sin, im * cos - re * sin
        result.append((re, im))
    return result


def gather_kernel(
    x_hbm, m_hbm, ct_hbm, ft_hbm, c_hbm, t_hbm, got, extra, taps_out, first, cm, tw,
    xs, ys, ms, ct, ft, ftt, early, tails, heads, sent, fir,
    load_sem, send_sem, recv_sem,
):
    me = place()
    mine = flat(me)
    barrier = pltpu.get_barrier_semaphore()
    for by in OTHERS:
        pl.semaphore_signal(barrier, inc=1, device_id=named(shifted(me, by)), device_id_type=MESH)
    loads = [
        pltpu.make_async_copy(x_hbm, xs.at[pl.ds(HEAD, ROWS)], load_sem.at[0]),
        pltpu.make_async_copy(ct_hbm, ct, load_sem.at[1]),
        pltpu.make_async_copy(m_hbm, ms, load_sem.at[2]),
        pltpu.make_async_copy(ft_hbm, ft, load_sem.at[3]),
        pltpu.make_async_copy(c_hbm, cm, load_sem.at[4]),
        pltpu.make_async_copy(t_hbm, tw, load_sem.at[5]),
    ]
    for load in loads:
        load.start()
    xs[pl.ds(0, HEAD), :] = jnp.zeros((HEAD, LANES), jnp.float32)
    xs[pl.ds(HEAD + ROWS, TAIL), :] = jnp.zeros((TAIL, LANES), jnp.float32)
    ys[pl.ds(0, HEAD), :] = jnp.zeros((HEAD, LANES), jnp.float32)
    loads[1].wait()
    taps = ct[...]
    taps = jnp.concatenate([taps, taps], axis=1)
    loads[0].wait()
    loads[2].wait()

    size = ROWS + TAIL
    left = lax.broadcasted_iota(jnp.int32, (size, LANES), 1) < CHANNELS
    here = xs[pl.ds(HEAD, size), :]
    before = xs[pl.ds(HEAD - 2, size), :]
    ys[pl.ds(HEAD, size), :] = pltpu.roll(jnp.where(left, here, before), CHANNELS, 1)

    def compute(a1):
        frames = [coarse_frames(xs, ys, taps, HALF * m + 2 * a1, LANES) for m in range(2)]
        result = spectra(ms, jnp.concatenate(frames, axis=0))
        sent[a1] = result.reshape(PEERS, 16, 256)

    def send(piece, source, target):
        copies = []
        for k, by in enumerate(OTHERS):
            to = shifted(me, by)
            copy = pltpu.make_async_remote_copy(
                src_ref=source.at[flat(to)],
                dst_ref=target.at[mine],
                send_sem=send_sem.at[piece, k],
                recv_sem=recv_sem.at[piece, k],
                device_id=named(to),
                device_id_type=MESH,
            )
            copy.start()
            copies.append(copy)
        return copies

    compute(0)
    early[mine] = sent[0, mine]
    pl.semaphore_wait(barrier, len(OTHERS))
    copies = [send(0, sent.at[0], early)]
    compute(1)
    got[mine] = sent[1, mine]
    copies.append(send(1, sent.at[1], got))

    ends = [coarse_frames(xs, ys, taps, ROWS + 2 * a1, 8) for a1 in range(2)]
    lower = lax.broadcasted_iota(jnp.int32, (8, 256), 0) < 4
    ends = jnp.where(lower, ends[0], pltpu.roll(ends[1], 4, 0))
    result = spectra(ms, jnp.concatenate([ends] * 16, axis=0))
    chosen = (
        lax.broadcasted_iota(jnp.int32, (16, LANES), 1) // 8
        == lax.broadcasted_iota(jnp.int32, (16, LANES), 0)
    )
    for d in range(PEERS):
        picked = jnp.where(chosen, result[16 * d : 16 * d + 16], 0.0)
        tails[d] = jnp.sum(picked, axis=0, keepdims=True)
    heads[mine] = tails[mine]
    copies.append(send(2, tails, heads))

    loads[3].wait()
    square = jnp.concatenate([ft[...], jnp.zeros((LANES - FINE_TAPS, FINE), jnp.float32)], axis=0)
    for k in range(4):
        ftt[pl.ds(LANES * k, LANES), :] = square[:, LANES * k : LANES * (k + 1)].T
    by_branch = [ftt[pl.ds(a, LANES, stride=4), :].T for a in range(4)]
    odd = lax.rem(lax.broadcasted_iota(jnp.int32, (8, LANES), 0), 2) == 1
    for a1 in range(2):
        for j in range(FINE_TAPS):
            even_row = jnp.broadcast_to(by_branch[2 * a1][j : j + 1], (8, LANES))
            odd_row = jnp.broadcast_to(by_branch[2 * a1 + 1][j : j + 1], (8, LANES))
            taps_out[a1, j] = jnp.where(odd, odd_row, even_row)
    loads[4].wait()
    loads[5].wait()

    for copy in copies[2]:
        copy.wait_recv()
    spread = jnp.concatenate(
        [jnp.where(chosen, jnp.broadcast_to(heads[s], (16, LANES)), 0.0) for s in range(PEERS)],
        axis=0,
    )
    row = lax.rem(lax.broadcasted_iota(jnp.int32, (256, 256), 0), 8)
    column = lax.broadcasted_iota(jnp.int32, (256, 256), 1)
    lane = lax.rem(column, LANES)
    select = jnp.logical_and(lane < 4, row == column // LANES * 4 + lane)
    added = jnp.dot(
        jnp.concatenate(split(spread), axis=1),
        jnp.where(select, 1.0, 0.0).astype(jnp.bfloat16),
        preferred_element_type=jnp.float32,
    )
    extra[...] = added[:, LANES:].reshape(PEERS, 16, LANES)

    for copy in copies[0]:
        copy.wait_recv()
    for s in range(1, PEERS):
        early[s, :, 0:LANES] += added[16 * s - 16 : 16 * s, :LANES]
    fine_filter(
        0,
        lambda c, f: early[f // 2, pl.ds(8 * c, 8), pl.ds(LANES * (f % 2), LANES)],
        lambda j: taps_out[0, j],
        fir,
    )
    for k in range(4):
        for h, parts in enumerate(fine_spectra(0, k, fir, cm, tw)):
            for c in range(2):
                first[k, h, c] = parts[c]

    for copy in copies[1]:
        copy.wait_recv()
    for piece in copies:
        for copy in piece:
            copy.wait_send()


def fine_kernel(got, extra, taps, first, cm, tw, out, fir, stage, out_sem):
    blocks = {}

    def block(c, frame):
        if (c, frame) not in blocks:
            value = got[frame // 2, pl.ds(8 * c, 8), pl.ds(LANES * (frame % 2), LANES)]
            if frame % 2 == 0 and frame > 0:
                value = value + extra[frame // 2 - 1, pl.ds(8 * c, 8), :]
            blocks[c, frame] = value
        return blocks[c, frame]

    fine_filter(1, block, lambda j: taps[1, j], fir)
    writes = []
    for k in range(4):
        (re1, im1), (re3, im3) = fine_spectra(1, k, fir, cm, tw)
        re0, im0, re2, im2 = first[k, 0, 0], first[k, 0, 1], re1, im1
        re1, im1 = first[k, 1, 0], first[k, 1, 1]
        sum_re, sum_im = re0 + re2, im0 + im2
        dif_re, dif_im = re0 - re2, im0 - im2
        odd_re, odd_im = re1 + re3, im1 + im3
        off_re, off_im = re1 - re3, im1 - im3
        stage[k, 0, :, 0:128] = sum_re + odd_re
        stage[k, 1, :, 0:128] = sum_im + odd_im
        stage[k, 0, :, 128:256] = dif_re + off_im
        stage[k, 1, :, 128:256] = dif_im - off_re
        stage[k, 0, :, 256:384] = sum_re - odd_re
        stage[k, 1, :, 256:384] = sum_im - odd_im
        stage[k, 0, :, 384:512] = dif_re - off_im
        stage[k, 1, :, 384:512] = dif_im + off_re
        for c in range(2):
            write = pltpu.make_async_copy(stage.at[k, c], out.at[c, k], out_sem.at[k, c])
            write.start()
            writes.append(write)
    for write in writes:
        write.wait()


def on_device(signal, coarse_taps, fine_taps):
    rows = signal.reshape(2, HALF, LANES).transpose(1, 0, 2).reshape(ROWS, LANES)
    hbm = pl.BlockSpec(memory_space=pltpu.HBM)
    vmem = pl.BlockSpec(memory_space=pltpu.VMEM)
    tables = [jnp.asarray(v) for v in (coarse_matrix(), fine_matrix(), twiddles())]
    operands = (rows, tables[0], coarse_taps, fine_taps, *tables[1:])
    f32 = jnp.float32
    handed = pl.pallas_call(
        gather_kernel,
        out_shape=[
            jax.ShapeDtypeStruct((PEERS, 16, 256), f32),
            jax.ShapeDtypeStruct((PEERS, 16, LANES), f32),
            jax.ShapeDtypeStruct((2, FINE_TAPS, 8, LANES), f32),
            jax.ShapeDtypeStruct((4, 2, 2, 32, LANES), f32),
            jax.ShapeDtypeStruct((768, 256), jnp.bfloat16),
            jax.ShapeDtypeStruct((8, LANES), f32),
        ],
        in_specs=[hbm] * 6,
        out_specs=[vmem] * 6,
        scratch_shapes=[
            pltpu.VMEM((HEAD + ROWS + TAIL, LANES), f32),
            pltpu.VMEM((HEAD + ROWS + TAIL, LANES), f32),
            pltpu.VMEM((256, 768), jnp.bfloat16),
            pltpu.VMEM((TAPS, CHANNELS), f32),
            pltpu.VMEM((FINE_TAPS, FINE), f32),
            pltpu.VMEM((FINE, LANES), f32),
            pltpu.VMEM((PEERS, 16, 256), f32),
            pltpu.VMEM((PEERS, 1, LANES), f32),
            pltpu.VMEM((PEERS, 1, LANES), f32),
            pltpu.VMEM((2, PEERS, 16, 256), f32),
            pltpu.VMEM((2, 256, LANES), f32),
            pltpu.SemaphoreType.DMA((6,)),
            pltpu.SemaphoreType.DMA((3, len(OTHERS))),
            pltpu.SemaphoreType.DMA((3, len(OTHERS))),
        ],
        compiler_params=pltpu.CompilerParams(
            collective_id=0, has_side_effects=True, vmem_limit_bytes=16 << 20
        ),
        name="gather",
    )(*(pltpu.with_memory_space_constraint(v, pltpu.HBM) for v in operands))
    return pl.pallas_call(
        fine_kernel,
        out_shape=jax.ShapeDtypeStruct((2, 4, 32, FINE), f32),
        in_specs=[vmem] * 6,
        out_specs=hbm,
        scratch_shapes=[
            pltpu.VMEM((2, 256, LANES), f32),
            pltpu.VMEM((4, 2, 32, FINE), f32),
            pltpu.SemaphoreType.DMA((4, 2)),
        ],
        compiler_params=pltpu.CompilerParams(vmem_limit_bytes=16 << 20),
        name="fine",
    )(*handed)


def solution(mesh):
    finer = Mesh(mesh.devices.reshape(mesh.shape["streams"], *GROUP), ("streams", *TM))
    return jax.shard_map(
        on_device,
        mesh=finer,
        in_specs=(P(None, ("streams", *TM)), P(), P()),
        out_specs=P(None, TM, "streams", None),
        check_vma=False,
    )
```

time: 31.1 us -> 26.2 us (0.84)
  the two profiles are of different devices: /device:TPU:1 before, /device:TPU:32 now
where the time goes in v2:
time: 26.2 us; the launch traced here: 26.1 us
  Pallas kernels  26.1 us (100%)
    pallas_call x1, Pallas kernels, on_device(): pl.pallas_call(gather_kernel, out_shape=[jax.ShapeDtypeStruct((PEERS, 16,...  24.8 us
    pallas_call x1, Pallas kernels, on_device(): pl.pallas_call(fine_kernel, out_shape=jax.ShapeDtypeStruct((2, 4, 32, FIN...  1.32 us

profile of v2, /device:TPU:32, one launch (start us, length us, event | category | flops | bytes accessed | tf_op | source)
XLA Modules:
  0.0 26.1 jit_solution(8070185925037400783)
XLA Ops:
  0.0 24.8 %gather.1 = (f32[16,16,256]{2,1,0:T(8,128)S(1)}, f32[16,16,128]{2,1,0:T(8,128)S(1)}, f32[2,12,8,128]{3,2,1,0:T(8,128)S(1)}, f32[4,2,2,32,128]{4,3,2,1,0:T(8,128)...) custom-call(f32[1024,128]{1,0:T(8,128)} %bitcast.5, bf16[256,768]{1,0:T(8,128)(2,1)} %constant.6.clone.m_hbm, ...), custom_call_target="tpu_custom_call" | custom-call | tf_op jit(solution)/shard_map/gather/pallas_call | solution.py:323
  24.8 1.3 %fine.1 = f32[2,4,32,512]{3,2,1,0:T(8,128)} custom-call(f32[16,16,256]{2,1,0:T(8,128)S(1)} %get-tuple-element.11.got, f32[16,16,128]{2,1,0:T(8,128)S(1)} %get-tuple-element.12.extra, f32[2,12,8,128]{3,2,1,0:T(8,128)S(1)} %get-tuple-element.13.taps, f32[4,2,2,32,128]{4,3,2,1,0:T(8,128)S(1)} %get-tuple-element.14.first, ...), custom_call_target="tpu_custom_call" | custom-call | tf_op jit(solution)/shard_map/fine/pallas_call | solution.py:356

commit v3 on v2

--- a/solution.py
+++ b/solution.py
@@ -23,13 +23,8 @@
 ROWS = 1024
 HALF = 512
 MESH = pl.DeviceIdType.MESH
-OTHERS = [
-    (dz, dy, dc)
-    for dz in (1, 0)
-    for dy in (2, 1, 3, 0)
-    for dc in (1, 0)
-    if (dz, dy, dc) != (0, 0, 0)
-]
+ACROSS = [(y, c) for y in (0, 1, 3, 2) for c in (1, 0)]
+BESIDE = [(dy, dc) for dy in (2, 1, 3, 0) for dc in (1, 0) if (dy, dc) != (0, 0)]
 
 
 def split(value):
@@ -78,20 +73,12 @@
     return np.concatenate([np.cos(angle), np.sin(angle)]).astype(np.float32)
 
 
-def place():
-    return tuple(lax.axis_index(a) for a in TM)
-
-
-def shifted(me, by):
-    return tuple(lax.rem(m + d, n) for m, d, n in zip(me, by, GROUP, strict=True))
-
-
-def flat(at):
-    return (at[0] * 4 + at[1]) * 2 + at[2]
-
-
-def named(at):
-    return dict(zip(TM, at, strict=True))
+def flat(zh, y, c):
+    return (zh * 4 + y) * 2 + c
+
+
+def named(zh, y, c):
+    return {"zh": zh, "y": y, "c": c}
 
 
 def coarse_frames(xs, ys, taps, start, size):
@@ -148,13 +135,17 @@
 def gather_kernel(
     x_hbm, m_hbm, ct_hbm, ft_hbm, c_hbm, t_hbm, got, extra, taps_out, first, cm, tw,
     xs, ys, ms, ct, ft, ftt, early, tails, heads, sent, fir,
-    load_sem, send_sem, recv_sem,
+    load_sem, send_sem, recv_sem, ready, again,
 ):
-    me = place()
-    mine = flat(me)
+    zh, y, c = (lax.axis_index(axis) for axis in TM)
+    mine = flat(zh, y, c)
+    own = 2 * y + c
+    other = 1 - zh
+    late = zh == 1
+    held = jnp.logical_and(late, lax.axis_index("streams") // 4 == 3)
     barrier = pltpu.get_barrier_semaphore()
-    for by in OTHERS:
-        pl.semaphore_signal(barrier, inc=1, device_id=named(shifted(me, by)), device_id_type=MESH)
+    for at in ACROSS:
+        pl.semaphore_signal(barrier, inc=1, device_id=named(other, *at), device_id_type=MESH)
     loads = [
         pltpu.make_async_copy(x_hbm, xs.at[pl.ds(HEAD, ROWS)], load_sem.at[0]),
         pltpu.make_async_copy(ct_hbm, ct, load_sem.at[1]),
@@ -165,6 +156,15 @@
     ]
     for load in loads:
         load.start()
+
+    @pl.when(late)
+    def _():
+        pl.semaphore_wait(barrier, len(ACROSS))
+        for at in ACROSS:
+            pl.semaphore_signal(
+                ready.at[own], inc=1, device_id=named(other, *at), device_id_type=MESH
+            )
+
     xs[pl.ds(0, HEAD), :] = jnp.zeros((HEAD, LANES), jnp.float32)
     xs[pl.ds(HEAD + ROWS, TAIL), :] = jnp.zeros((TAIL, LANES), jnp.float32)
     ys[pl.ds(0, HEAD), :] = jnp.zeros((HEAD, LANES), jnp.float32)
@@ -185,29 +185,61 @@
         result = spectra(ms, jnp.concatenate(frames, axis=0))
         sent[a1] = result.reshape(PEERS, 16, 256)
 
-    def send(piece, source, target):
+    def crossing(piece, source, target):
+        return [
+            pltpu.make_async_remote_copy(
+                src_ref=source.at[flat(other, *at)],
+                dst_ref=target.at[mine],
+                send_sem=send_sem.at[piece, flat(0, *at)],
+                recv_sem=recv_sem.at[piece, own],
+                device_id=named(other, *at),
+                device_id_type=MESH,
+            )
+            for at in ACROSS
+        ]
+
+    def staying(piece, source, target):
         copies = []
-        for k, by in enumerate(OTHERS):
-            to = shifted(me, by)
+        for k, (dy, dc) in enumerate(BESIDE):
+            to = (zh, lax.rem(y + dy, 4), lax.rem(c + dc, 2))
             copy = pltpu.make_async_remote_copy(
-                src_ref=source.at[flat(to)],
+                src_ref=source.at[flat(*to)],
                 dst_ref=target.at[mine],
+                send_sem=send_sem.at[piece, 8 + k],
+                recv_sem=recv_sem.at[piece, 8 + k],
+                device_id=named(*to),
+                device_id_type=MESH,
+            )
+            copies.append(copy)
+        return copies
+
+    def arrived(piece, target, first, count):
+        for k in range(first, first + count):
+            pltpu.make_async_remote_copy(
+                src_ref=target.at[0],
+                dst_ref=target.at[0],
                 send_sem=send_sem.at[piece, k],
                 recv_sem=recv_sem.at[piece, k],
-                device_id=named(to),
+                device_id=named(other, y, c),
                 device_id_type=MESH,
-            )
-            copy.start()
-            copies.append(copy)
-        return copies
+            ).wait_recv()
 
     compute(0)
+    zero = crossing(0, sent.at[0], early)
+    for at, copy in zip(ACROSS, zero, strict=True):
+
+        @pl.when(jnp.logical_not(late))
+        def _():
+            pl.semaphore_wait(ready.at[flat(0, *at)], 1)
+
+        copy.start()
+
+    @pl.when(jnp.logical_not(late))
+    def _():
+        pl.semaphore_wait(barrier, len(ACROSS))
+        pl.semaphore_signal(again, inc=1, device_id=named(other, y, c), device_id_type=MESH)
+
     early[mine] = sent[0, mine]
-    pl.semaphore_wait(barrier, len(OTHERS))
-    copies = [send(0, sent.at[0], early)]
-    compute(1)
-    got[mine] = sent[1, mine]
-    copies.append(send(1, sent.at[1], got))
 
     ends = [coarse_frames(xs, ys, taps, ROWS + 2 * a1, 8) for a1 in range(2)]
     lower = lax.broadcasted_iota(jnp.int32, (8, 256), 0) < 4
@@ -221,7 +253,30 @@
         picked = jnp.where(chosen, result[16 * d : 16 * d + 16], 0.0)
         tails[d] = jnp.sum(picked, axis=0, keepdims=True)
     heads[mine] = tails[mine]
-    copies.append(send(2, tails, heads))
+    two = crossing(2, tails, heads)
+    for copy in two:
+        copy.start()
+
+    compute(1)
+    got[mine] = sent[1, mine]
+    one = crossing(1, sent.at[1], got)
+
+    @pl.when(jnp.logical_not(held))
+    def _():
+        for copy in one:
+            copy.start()
+
+    @pl.when(late)
+    def _():
+        pl.semaphore_wait(again, 1)
+
+    near = [
+        *staying(0, sent.at[0], early),
+        *staying(2, tails, heads),
+        *staying(1, sent.at[1], got),
+    ]
+    for copy in near:
+        copy.start()
 
     loads[3].wait()
     square = jnp.concatenate([ft[...], jnp.zeros((LANES - FINE_TAPS, FINE), jnp.float32)], axis=0)
@@ -237,8 +292,15 @@
     loads[4].wait()
     loads[5].wait()
 
-    for copy in copies[2]:
-        copy.wait_recv()
+    arrived(0, early, 0, 8)
+
+    @pl.when(held)
+    def _():
+        for copy in one:
+            copy.start()
+
+    arrived(0, early, 8, 7)
+    arrived(2, heads, 0, 15)
     spread = jnp.concatenate(
         [jnp.where(chosen, jnp.broadcast_to(heads[s], (16, LANES)), 0.0) for s in range(PEERS)],
         axis=0,
@@ -254,8 +316,6 @@
     )
     extra[...] = added[:, LANES:].reshape(PEERS, 16, LANES)
 
-    for copy in copies[0]:
-        copy.wait_recv()
     for s in range(1, PEERS):
         early[s, :, 0:LANES] += added[16 * s - 16 : 16 * s, :LANES]
     fine_filter(
@@ -269,11 +329,9 @@
             for c in range(2):
                 first[k, h, c] = parts[c]
 
-    for copy in copies[1]:
-        copy.wait_recv()
-    for piece in copies:
-        for copy in piece:
-            copy.wait_send()
+    arrived(1, got, 0, 15)
+    for copy in (*zero, *two, *one, *near):
+        copy.wait_send()
 
 
 def fine_kernel(got, extra, taps, first, cm, tw, out, fir, stage, out_sem):
@@ -345,8 +403,10 @@
             pltpu.VMEM((2, PEERS, 16, 256), f32),
             pltpu.VMEM((2, 256, LANES), f32),
             pltpu.SemaphoreType.DMA((6,)),
-            pltpu.SemaphoreType.DMA((3, len(OTHERS))),
-            pltpu.SemaphoreType.DMA((3, len(OTHERS))),
+            pltpu.SemaphoreType.DMA((3, 15)),
+            pltpu.SemaphoreType.DMA((3, 15)),
+            pltpu.SemaphoreType.REGULAR((8,)),
+            pltpu.SemaphoreType.REGULAR,
         ],
         compiler_params=pltpu.CompilerParams(
             collective_id=0, has_side_effects=True, vmem_limit_bytes=16 << 20

time: 26.2 us -> 29.5 us (1.13)
  the two profiles are of different devices: /device:TPU:32 before, /device:TPU:102 now
where the time goes in v3:
time: 29.5 us; the launch traced here: 29.4 us
  Pallas kernels  29.4 us (100%)
    pallas_call x1, Pallas kernels, on_device(): pl.pallas_call(gather_kernel, out_shape=[jax.ShapeDtypeStruct((PEERS, 16,...  28.1 us
    pallas_call x1, Pallas kernels, on_device(): pl.pallas_call(fine_kernel, out_shape=jax.ShapeDtypeStruct((2, 4, 32, FIN...  1.32 us

profile of v3, /device:TPU:102, one launch (start us, length us, event | category | flops | bytes accessed | tf_op | source)
XLA Modules:
  0.0 29.4 jit_solution(4029258276165385981)
XLA Ops:
  0.0 28.1 %gather.1 = (f32[16,16,256]{2,1,0:T(8,128)S(1)}, f32[16,16,128]{2,1,0:T(8,128)S(1)}, f32[2,12,8,128]{3,2,1,0:T(8,128)S(1)}, f32[4,2,2,32,128]{4,3,2,1,0:T(8,128)...) custom-call(f32[1024,128]{1,0:T(8,128)} %bitcast.5, bf16[256,768]{1,0:T(8,128)(2,1)} %constant.6.clone.m_hbm, ...), custom_call_target="tpu_custom_call" | custom-call | tf_op jit(solution)/shard_map/gather/pallas_call | solution.py:381
  28.1 1.3 %fine.1 = f32[2,4,32,512]{3,2,1,0:T(8,128)} custom-call(f32[16,16,256]{2,1,0:T(8,128)S(1)} %get-tuple-element.11.got, f32[16,16,128]{2,1,0:T(8,128)S(1)} %get-tuple-element.12.extra, f32[2,12,8,128]{3,2,1,0:T(8,128)S(1)} %get-tuple-element.13.taps, f32[4,2,2,32,128]{4,3,2,1,0:T(8,128)S(1)} %get-tuple-element.14.first, ...), custom_call_target="tpu_custom_call" | custom-call | tf_op jit(solution)/shard_map/fine/pallas_call | solution.py:416

commit v4 on v3

--- a/solution.py
+++ b/solution.py
@@ -23,7 +23,6 @@
 ROWS = 1024
 HALF = 512
 MESH = pl.DeviceIdType.MESH
-ACROSS = [(y, c) for y in (0, 1, 3, 2) for c in (1, 0)]
 BESIDE = [(dy, dc) for dy in (2, 1, 3, 0) for dc in (1, 0) if (dy, dc) != (0, 0)]
 
 
@@ -53,8 +52,7 @@
     angle = 2.0 * np.pi * (channel * branch % CHANNELS) / CHANNELS
     value = np.where(part == part_in, np.cos(angle), np.sin(angle) * (part_in - part))
     value = np.where(parity == parity_in, value, 0.0) / math.sqrt(CHANNELS)
-    high, low = np_split(value)
-    return np.concatenate([high, low, high], axis=1)
+    return np.concatenate(np_split(value), axis=1)
 
 
 def fine_matrix():
@@ -96,9 +94,11 @@
 
 def spectra(ms, frames):
     high, low = split(frames)
-    right = jnp.concatenate([high, high, low], axis=1)
-    return lax.dot_general(
-        ms[...], right, (((1,), (1,)), ((), ())), preferred_element_type=jnp.float32
+    dims = (((1,), (1,)), ((), ()))
+    right = jnp.concatenate([high, high], axis=1)
+    result = lax.dot_general(ms[...], right, dims, preferred_element_type=jnp.float32)
+    return result + lax.dot_general(
+        ms[:, 0:256], low, dims, preferred_element_type=jnp.float32
     )
 
 
@@ -137,30 +137,37 @@
     xs, ys, ms, ct, ft, ftt, early, tails, heads, sent, fir,
     load_sem, send_sem, recv_sem, ready, again,
 ):
+    loads = [
+        pltpu.make_async_copy(ct_hbm, ct, load_sem.at[0]),
+        pltpu.make_async_copy(
+            x_hbm.at[pl.ds(0, HALF)], xs.at[pl.ds(HEAD, HALF)], load_sem.at[1]
+        ),
+        pltpu.make_async_copy(
+            x_hbm.at[pl.ds(HALF, HALF)], xs.at[pl.ds(HEAD + HALF, HALF)], load_sem.at[2]
+        ),
+        pltpu.make_async_copy(m_hbm, ms, load_sem.at[3]),
+        pltpu.make_async_copy(ft_hbm, ft, load_sem.at[4]),
+        pltpu.make_async_copy(c_hbm, cm, load_sem.at[5]),
+        pltpu.make_async_copy(t_hbm, tw, load_sem.at[6]),
+    ]
+    for load in loads[:4]:
+        load.start()
     zh, y, c = (lax.axis_index(axis) for axis in TM)
     mine = flat(zh, y, c)
     own = 2 * y + c
     other = 1 - zh
     late = zh == 1
-    held = jnp.logical_and(late, lax.axis_index("streams") // 4 == 3)
+    turn = lax.rem(lax.div(y + 1, 2), 2)
+    odd_y = lax.rem(y, 2)
+    across = [(dy, dc) for dy in (turn, 1 - turn, 3 - odd_y, 2 + odd_y) for dc in (1, 0)]
     barrier = pltpu.get_barrier_semaphore()
-    for at in ACROSS:
+    for at in across:
         pl.semaphore_signal(barrier, inc=1, device_id=named(other, *at), device_id_type=MESH)
-    loads = [
-        pltpu.make_async_copy(x_hbm, xs.at[pl.ds(HEAD, ROWS)], load_sem.at[0]),
-        pltpu.make_async_copy(ct_hbm, ct, load_sem.at[1]),
-        pltpu.make_async_copy(m_hbm, ms, load_sem.at[2]),
-        pltpu.make_async_copy(ft_hbm, ft, load_sem.at[3]),
-        pltpu.make_async_copy(c_hbm, cm, load_sem.at[4]),
-        pltpu.make_async_copy(t_hbm, tw, load_sem.at[5]),
-    ]
-    for load in loads:
-        load.start()
 
     @pl.when(late)
     def _():
-        pl.semaphore_wait(barrier, len(ACROSS))
-        for at in ACROSS:
+        pl.semaphore_wait(barrier, 8)
+        for at in across:
             pl.semaphore_signal(
                 ready.at[own], inc=1, device_id=named(other, *at), device_id_type=MESH
             )
@@ -168,78 +175,94 @@
     xs[pl.ds(0, HEAD), :] = jnp.zeros((HEAD, LANES), jnp.float32)
     xs[pl.ds(HEAD + ROWS, TAIL), :] = jnp.zeros((TAIL, LANES), jnp.float32)
     ys[pl.ds(0, HEAD), :] = jnp.zeros((HEAD, LANES), jnp.float32)
-    loads[1].wait()
+    loads[0].wait()
     taps = ct[...]
     taps = jnp.concatenate([taps, taps], axis=1)
-    loads[0].wait()
-    loads[2].wait()
-
-    size = ROWS + TAIL
-    left = lax.broadcasted_iota(jnp.int32, (size, LANES), 1) < CHANNELS
-    here = xs[pl.ds(HEAD, size), :]
-    before = xs[pl.ds(HEAD - 2, size), :]
-    ys[pl.ds(HEAD, size), :] = pltpu.roll(jnp.where(left, here, before), CHANNELS, 1)
-
-    def compute(a1):
-        frames = [coarse_frames(xs, ys, taps, HALF * m + 2 * a1, LANES) for m in range(2)]
-        result = spectra(ms, jnp.concatenate(frames, axis=0))
-        sent[a1] = result.reshape(PEERS, 16, 256)
+
+    def delay(start, size):
+        left = lax.broadcasted_iota(jnp.int32, (size, LANES), 1) < CHANNELS
+        here = xs[pl.ds(start, size), :]
+        before = xs[pl.ds(start - 2, size), :]
+        ys[pl.ds(start, size), :] = pltpu.roll(jnp.where(left, here, before), CHANNELS, 1)
+
+    def compute(a1, m):
+        frames = coarse_frames(xs, ys, taps, HALF * m + 2 * a1, LANES)
+        sent[a1, :, :, LANES * m : LANES * (m + 1)] = spectra(ms, frames).reshape(
+            PEERS, 16, LANES
+        )
 
     def crossing(piece, source, target):
         return [
             pltpu.make_async_remote_copy(
                 src_ref=source.at[flat(other, *at)],
                 dst_ref=target.at[mine],
-                send_sem=send_sem.at[piece, flat(0, *at)],
-                recv_sem=recv_sem.at[piece, own],
+                send_sem=send_sem.at[piece],
+                recv_sem=recv_sem.at[piece],
                 device_id=named(other, *at),
                 device_id_type=MESH,
             )
-            for at in ACROSS
+            for at in across
         ]
 
     def staying(piece, source, target):
         copies = []
-        for k, (dy, dc) in enumerate(BESIDE):
+        for dy, dc in BESIDE:
             to = (zh, lax.rem(y + dy, 4), lax.rem(c + dc, 2))
             copy = pltpu.make_async_remote_copy(
                 src_ref=source.at[flat(*to)],
                 dst_ref=target.at[mine],
-                send_sem=send_sem.at[piece, 8 + k],
-                recv_sem=recv_sem.at[piece, 8 + k],
+                send_sem=send_sem.at[piece],
+                recv_sem=recv_sem.at[piece],
                 device_id=named(*to),
                 device_id_type=MESH,
             )
             copies.append(copy)
         return copies
 
-    def arrived(piece, target, first, count):
-        for k in range(first, first + count):
-            pltpu.make_async_remote_copy(
-                src_ref=target.at[0],
-                dst_ref=target.at[0],
-                send_sem=send_sem.at[piece, k],
-                recv_sem=recv_sem.at[piece, k],
-                device_id=named(other, y, c),
-                device_id_type=MESH,
-            ).wait_recv()
-
-    compute(0)
+    def whole(piece, source, target):
+        return pltpu.make_async_remote_copy(
+            src_ref=source.at[pl.ds(0, 15)],
+            dst_ref=target.at[pl.ds(0, 15)],
+            send_sem=send_sem.at[piece],
+            recv_sem=recv_sem.at[piece],
+            device_id=named(other, y, c),
+            device_id_type=MESH,
+        )
+
+    def part(m, at):
+        return pltpu.make_async_remote_copy(
+            src_ref=sent.at[0, flat(other, *at), :, pl.ds(LANES * m, LANES)],
+            dst_ref=early.at[mine, :, pl.ds(LANES * m, LANES)],
+            send_sem=send_sem.at[0],
+            recv_sem=recv_sem.at[0],
+            device_id=named(other, *at),
+            device_id_type=MESH,
+        )
+
     zero = crossing(0, sent.at[0], early)
-    for at, copy in zip(ACROSS, zero, strict=True):
-
-        @pl.when(jnp.logical_not(late))
+    one = crossing(1, sent.at[1], got)
+    two = crossing(2, tails, heads)
+
+    def start(copies):
+        @pl.when(late)
         def _():
-            pl.semaphore_wait(ready.at[flat(0, *at)], 1)
-
-        copy.start()
-
-    @pl.when(jnp.logical_not(late))
-    def _():
-        pl.semaphore_wait(barrier, len(ACROSS))
-        pl.semaphore_signal(again, inc=1, device_id=named(other, y, c), device_id_type=MESH)
-
-    early[mine] = sent[0, mine]
+            for copy in copies:
+                copy.start()
+
+    loads[1].wait()
+    delay(HEAD, HALF)
+    loads[3].wait()
+    compute(0, 0)
+    start([part(0, at) for at in across[:4]])
+    loads[2].wait()
+    delay(HEAD + HALF, HALF + TAIL)
+    compute(0, 1)
+    start([part(1, at) for at in across[:4]])
+    for load in loads[4:]:
+        load.start()
+    compute(1, 0)
+    compute(1, 1)
+    start(one[:4])
 
     ends = [coarse_frames(xs, ys, taps, ROWS + 2 * a1, 8) for a1 in range(2)]
     lower = lax.broadcasted_iota(jnp.int32, (8, 256), 0) < 4
@@ -253,18 +276,21 @@
         picked = jnp.where(chosen, result[16 * d : 16 * d + 16], 0.0)
         tails[d] = jnp.sum(picked, axis=0, keepdims=True)
     heads[mine] = tails[mine]
-    two = crossing(2, tails, heads)
-    for copy in two:
-        copy.start()
-
-    compute(1)
+    start([*two, *zero[4:], *one[4:]])
+
+    @pl.when(jnp.logical_not(late))
+    def _():
+        for half in (slice(0, 4), slice(4, 8)):
+            for at, copy in zip(across[half], zero[half], strict=True):
+                pl.semaphore_wait(ready.at[flat(0, *at)], 1)
+                copy.start()
+            for copy in (*two[half], *one[half]):
+                copy.start()
+        pl.semaphore_wait(barrier, 8)
+        pl.semaphore_signal(again, inc=1, device_id=named(other, y, c), device_id_type=MESH)
+
+    early[mine] = sent[0, mine]
     got[mine] = sent[1, mine]
-    one = crossing(1, sent.at[1], got)
-
-    @pl.when(jnp.logical_not(held))
-    def _():
-        for copy in one:
-            copy.start()
 
     @pl.when(late)
     def _():
@@ -278,7 +304,7 @@
     for copy in near:
         copy.start()
 
-    loads[3].wait()
+    loads[4].wait()
     square = jnp.concatenate([ft[...], jnp.zeros((LANES - FINE_TAPS, FINE), jnp.float32)], axis=0)
     for k in range(4):
         ftt[pl.ds(LANES * k, LANES), :] = square[:, LANES * k : LANES * (k + 1)].T
@@ -289,18 +315,12 @@
             even_row = jnp.broadcast_to(by_branch[2 * a1][j : j + 1], (8, LANES))
             odd_row = jnp.broadcast_to(by_branch[2 * a1 + 1][j : j + 1], (8, LANES))
             taps_out[a1, j] = jnp.where(odd, odd_row, even_row)
-    loads[4].wait()
     loads[5].wait()
-
-    arrived(0, early, 0, 8)
-
-    @pl.when(held)
-    def _():
-        for copy in one:
-            copy.start()
-
-    arrived(0, early, 8, 7)
-    arrived(2, heads, 0, 15)
+    loads[6].wait()
+
+    pieces = [whole(0, sent.at[0], early), whole(1, sent.at[1], got), whole(2, tails, heads)]
+    pieces[0].wait_recv()
+    pieces[2].wait_recv()
     spread = jnp.concatenate(
         [jnp.where(chosen, jnp.broadcast_to(heads[s], (16, LANES)), 0.0) for s in range(PEERS)],
         axis=0,
@@ -329,9 +349,9 @@
             for c in range(2):
                 first[k, h, c] = parts[c]
 
-    arrived(1, got, 0, 15)
-    for copy in (*zero, *two, *one, *near):
-        copy.wait_send()
+    pieces[0].wait_send()
+    pieces[2].wait_send()
+    pieces[1].wait()
 
 
 def fine_kernel(got, extra, taps, first, cm, tw, out, fir, stage, out_sem):
@@ -393,7 +413,7 @@
         scratch_shapes=[
             pltpu.VMEM((HEAD + ROWS + TAIL, LANES), f32),
             pltpu.VMEM((HEAD + ROWS + TAIL, LANES), f32),
-            pltpu.VMEM((256, 768), jnp.bfloat16),
+            pltpu.VMEM((256, 512), jnp.bfloat16),
             pltpu.VMEM((TAPS, CHANNELS), f32),
             pltpu.VMEM((FINE_TAPS, FINE), f32),
             pltpu.VMEM((FINE, LANES), f32),
@@ -402,9 +422,9 @@
             pltpu.VMEM((PEERS, 1, LANES), f32),
             pltpu.VMEM((2, PEERS, 16, 256), f32),
             pltpu.VMEM((2, 256, LANES), f32),
-            pltpu.SemaphoreType.DMA((6,)),
-            pltpu.SemaphoreType.DMA((3, 15)),
-            pltpu.SemaphoreType.DMA((3, 15)),
+            pltpu.SemaphoreType.DMA((7,)),
+            pltpu.SemaphoreType.DMA((3,)),
+            pltpu.SemaphoreType.DMA((3,)),
             pltpu.SemaphoreType.REGULAR((8,)),
             pltpu.SemaphoreType.REGULAR,
         ],

time: 29.5 us -> 23.3 us (0.79)
  the two profiles are of different devices: /device:TPU:102 before, /device:TPU:120 now
where the time goes in v4:
time: 23.3 us; the launch traced here: 23.1 us
  Pallas kernels  23.1 us (99%)
    pallas_call x1, Pallas kernels, on_device(): pl.pallas_call(gather_kernel, out_shape=[jax.ShapeDtypeStruct((PEERS, 16,...  21.8 us
    pallas_call x1, Pallas kernels, on_device(): pl.pallas_call(fine_kernel, out_shape=jax.ShapeDtypeStruct((2, 4, 32, FIN...  1.32 us

profile of v4, /device:TPU:120, one launch (start us, length us, event | category | flops | bytes accessed | tf_op | source)
XLA Modules:
  0.0 23.1 jit_solution(4771549113324881559)
XLA Ops:
  0.0 21.8 %gather.1 = (f32[16,16,256]{2,1,0:T(8,128)S(1)}, f32[16,16,128]{2,1,0:T(8,128)S(1)}, f32[2,12,8,128]{3,2,1,0:T(8,128)S(1)}, f32[4,2,2,32,128]{4,3,2,1,0:T(8,128)...) custom-call(f32[1024,128]{1,0:T(8,128)} %bitcast.5, bf16[256,512]{1,0:T(8,128)(2,1)} %constant.6.clone.m_hbm, ...), custom_call_target="tpu_custom_call" | custom-call | tf_op jit(solution)/shard_map/gather/pallas_call | solution.py:401
  21.8 1.3 %fine.1 = f32[2,4,32,512]{3,2,1,0:T(8,128)} custom-call(f32[16,16,256]{2,1,0:T(8,128)S(1)} %get-tuple-element.11.got, f32[16,16,128]{2,1,0:T(8,128)S(1)} %get-tuple-element.12.extra, f32[2,12,8,128]{3,2,1,0:T(8,128)S(1)} %get-tuple-element.13.taps, f32[4,2,2,32,128]{4,3,2,1,0:T(8,128)S(1)} %get-tuple-element.14.first, ...), custom_call_target="tpu_custom_call" | custom-call | tf_op jit(solution)/shard_map/fine/pallas_call | solution.py:436

commit v5 on v4

--- a/solution.py
+++ b/solution.py
@@ -102,39 +102,64 @@
     )
 
 
-def fine_filter(a1, block, taps, fir):
+def fine_filter(half, block, taps, fir):
     for c in range(2):
-        for frame in range(32):
+        blocks = {}
+        for frame in range(16 * half, 16 * half + 16):
             acc = None
             for j in range(min(FINE_TAPS, frame + 1)):
-                term = taps(j) * block(c, frame - j)
+                at = frame - j
+                if at not in blocks:
+                    blocks[at] = block(c, at)
+                term = taps(j) * blocks[at]
                 acc = term if acc is None else acc + term
-            fir[c, pl.ds(8 * frame, 8), :] = acc
-
-
-def fine_spectra(a1, k, fir, cm, tw):
+            fir[c, pl.ds(8 * (frame - 16 * half), 8), :] = acc
+
+
+def fine_spectra(a1, fir, cm, tw):
     rows = []
     for h in range(2):
-        parts = [fir[c, pl.ds(2 * k + h, 32, stride=8), :] for c in range(2)]
-        rows.append(jnp.concatenate(parts, axis=1))
+        for k in range(4):
+            parts = [fir[c, pl.ds(2 * k + h, 16, stride=8), :] for c in range(2)]
+            rows.append(jnp.concatenate(parts, axis=1))
     high, low = split(jnp.concatenate(rows, axis=0))
     left = jnp.concatenate([high, high, low], axis=1)
     spectrum = jnp.dot(left, cm[...], preferred_element_type=jnp.float32)
     result = []
     for h in range(2):
         a = 2 * a1 + h
-        re = spectrum[32 * h : 32 * h + 32, :LANES]
-        im = spectrum[32 * h : 32 * h + 32, LANES:]
+        re = spectrum[64 * h : 64 * h + 64, :LANES]
+        im = spectrum[64 * h : 64 * h + 64, LANES:]
         if a:
             cos, sin = tw[a : a + 1, :], tw[4 + a : 5 + a, :]
             re, im = re * cos + im * sin, im * cos - re * sin
         result.append((re, im))
-    return result
+    (re0, im0), (re1, im1) = result
+    quarters = [
+        (re0 + re1, im0 + im1),
+        (re0 + im1, im0 - re1),
+        (re0 - re1, im0 - im1),
+        (re0 - im1, im0 + re1),
+    ]
+    if a1:
+        quarters = [(-re, -im) if d % 2 else (re, im) for d, (re, im) in enumerate(quarters)]
+    return quarters
+
+
+def classes(a1, half, blocks, over_end, taps, fir, cm, tw):
+    def block(c, frame):
+        value = blocks[frame // 2, pl.ds(8 * c, 8), pl.ds(LANES * (frame % 2), LANES)]
+        if frame % 2 == 0 and frame > 0:
+            value = value + over_end[frame // 2 - 1, pl.ds(8 * c, 8), :]
+        return value
+
+    fine_filter(half, block, lambda j: taps[a1, j], fir)
+    return fine_spectra(a1, fir, cm, tw)
 
 
 def gather_kernel(
     x_hbm, m_hbm, ct_hbm, ft_hbm, c_hbm, t_hbm, got, extra, taps_out, first, cm, tw,
-    xs, ys, ms, ct, ft, ftt, early, tails, heads, sent, fir,
+    xs, ys, ms, ct, ft, ftt, early, tails, heads, sent, over_end, fir,
     load_sem, send_sem, recv_sem, ready, again,
 ):
     loads = [
@@ -157,6 +182,7 @@
     own = 2 * y + c
     other = 1 - zh
     late = zh == 1
+    patient = jnp.logical_and(zh == 0, lax.div(lax.axis_index("streams"), 4) == 1)
     turn = lax.rem(lax.div(y + 1, 2), 2)
     odd_y = lax.rem(y, 2)
     across = [(dy, dc) for dy in (turn, 1 - turn, 3 - odd_y, 2 + odd_y) for dc in (1, 0)]
@@ -190,6 +216,19 @@
         sent[a1, :, :, LANES * m : LANES * (m + 1)] = spectra(ms, frames).reshape(
             PEERS, 16, LANES
         )
+
+    def prepare():
+        loads[4].wait()
+        square = jnp.concatenate([ft[...], jnp.zeros((LANES - FINE_TAPS, FINE), jnp.float32)], axis=0)
+        for k in range(4):
+            ftt[pl.ds(LANES * k, LANES), :] = square[:, LANES * k : LANES * (k + 1)].T
+        by_branch = [ftt[pl.ds(a, LANES, stride=4), :].T for a in range(4)]
+        odd = lax.rem(lax.broadcasted_iota(jnp.int32, (8, LANES), 0), 2) == 1
+        for a1 in range(2):
+            for j in range(FINE_TAPS):
+                even_row = jnp.broadcast_to(by_branch[2 * a1][j : j + 1], (8, LANES))
+                odd_row = jnp.broadcast_to(by_branch[2 * a1 + 1][j : j + 1], (8, LANES))
+                taps_out[a1, j] = jnp.where(odd, odd_row, even_row)
 
     def crossing(piece, source, target):
         return [
@@ -212,19 +251,19 @@
                 src_ref=source.at[flat(*to)],
                 dst_ref=target.at[mine],
                 send_sem=send_sem.at[piece],
-                recv_sem=recv_sem.at[piece],
+                recv_sem=recv_sem.at[piece + 3],
                 device_id=named(*to),
                 device_id_type=MESH,
             )
             copies.append(copy)
         return copies
 
-    def whole(piece, source, target):
+    def whole(piece, target, count, near):
         return pltpu.make_async_remote_copy(
-            src_ref=source.at[pl.ds(0, 15)],
-            dst_ref=target.at[pl.ds(0, 15)],
+            src_ref=target.at[pl.ds(0, count)],
+            dst_ref=target.at[pl.ds(0, count)],
             send_sem=send_sem.at[piece],
-            recv_sem=recv_sem.at[piece],
+            recv_sem=recv_sem.at[piece + 3 * near],
             device_id=named(other, y, c),
             device_id_type=MESH,
         )
@@ -280,13 +319,21 @@
 
     @pl.when(jnp.logical_not(late))
     def _():
+        @pl.when(patient)
+        def _():
+            pl.semaphore_wait(barrier, 8)
+            prepare()
+
         for half in (slice(0, 4), slice(4, 8)):
             for at, copy in zip(across[half], zero[half], strict=True):
                 pl.semaphore_wait(ready.at[flat(0, *at)], 1)
                 copy.start()
             for copy in (*two[half], *one[half]):
                 copy.start()
-        pl.semaphore_wait(barrier, 8)
+        @pl.when(jnp.logical_not(patient))
+        def _():
+            pl.semaphore_wait(barrier, 8)
+
         pl.semaphore_signal(again, inc=1, device_id=named(other, y, c), device_id_type=MESH)
 
     early[mine] = sent[0, mine]
@@ -304,91 +351,104 @@
     for copy in near:
         copy.start()
 
-    loads[4].wait()
-    square = jnp.concatenate([ft[...], jnp.zeros((LANES - FINE_TAPS, FINE), jnp.float32)], axis=0)
-    for k in range(4):
-        ftt[pl.ds(LANES * k, LANES), :] = square[:, LANES * k : LANES * (k + 1)].T
-    by_branch = [ftt[pl.ds(a, LANES, stride=4), :].T for a in range(4)]
-    odd = lax.rem(lax.broadcasted_iota(jnp.int32, (8, LANES), 0), 2) == 1
-    for a1 in range(2):
-        for j in range(FINE_TAPS):
-            even_row = jnp.broadcast_to(by_branch[2 * a1][j : j + 1], (8, LANES))
-            odd_row = jnp.broadcast_to(by_branch[2 * a1 + 1][j : j + 1], (8, LANES))
-            taps_out[a1, j] = jnp.where(odd, odd_row, even_row)
+    @pl.when(jnp.logical_not(patient))
+    def _():
+        prepare()
+
     loads[5].wait()
     loads[6].wait()
 
-    pieces = [whole(0, sent.at[0], early), whole(1, sent.at[1], got), whole(2, tails, heads)]
-    pieces[0].wait_recv()
-    pieces[2].wait_recv()
-    spread = jnp.concatenate(
-        [jnp.where(chosen, jnp.broadcast_to(heads[s], (16, LANES)), 0.0) for s in range(PEERS)],
-        axis=0,
-    )
+    def wait_for(count, near):
+        whole(0, early, count, near).wait_recv()
+        whole(2, heads, count, near).wait_recv()
+
     row = lax.rem(lax.broadcasted_iota(jnp.int32, (256, 256), 0), 8)
     column = lax.broadcasted_iota(jnp.int32, (256, 256), 1)
     lane = lax.rem(column, LANES)
     select = jnp.logical_and(lane < 4, row == column // LANES * 4 + lane)
-    added = jnp.dot(
-        jnp.concatenate(split(spread), axis=1),
-        jnp.where(select, 1.0, 0.0).astype(jnp.bfloat16),
-        preferred_element_type=jnp.float32,
-    )
-    extra[...] = added[:, LANES:].reshape(PEERS, 16, LANES)
-
-    for s in range(1, PEERS):
-        early[s, :, 0:LANES] += added[16 * s - 16 : 16 * s, :LANES]
-    fine_filter(
-        0,
-        lambda c, f: early[f // 2, pl.ds(8 * c, 8), pl.ds(LANES * (f % 2), LANES)],
-        lambda j: taps_out[0, j],
-        fir,
-    )
-    for k in range(4):
-        for h, parts in enumerate(fine_spectra(0, k, fir, cm, tw)):
-            for c in range(2):
-                first[k, h, c] = parts[c]
-
-    pieces[0].wait_send()
-    pieces[2].wait_send()
-    pieces[1].wait()
+    select = jnp.where(select, 1.0, 0.0).astype(jnp.bfloat16)
+
+    def spread(half):
+        some = slice(8 * half, 8 * half + 8)
+        picked = [
+            jnp.where(chosen, jnp.broadcast_to(heads[s], (16, LANES)), 0.0)
+            for s in range(8 * half, 8 * half + 8)
+        ]
+        added = jnp.dot(
+            jnp.concatenate(split(jnp.concatenate(picked, axis=0)), axis=1),
+            select,
+            preferred_element_type=jnp.float32,
+        ).reshape(8, 16, 256)
+        over_end[some] = added[:, :, :LANES]
+        extra[some] = added[:, :, LANES:]
+
+    def put(half, quarters, add):
+        rows = slice(16 * half, 16 * half + 16)
+        for d, both in enumerate(quarters):
+            lanes = slice(LANES * d, LANES * d + LANES)
+            for part, value in enumerate(both):
+                value = value.reshape(4, 16, LANES)
+                if add:
+                    value = value + first[part, :, rows, lanes]
+                first[part, :, rows, lanes] = value
+
+    wait_for(7, True)
+    whole(1, got, 7, True).wait_recv()
+
+    @pl.when(late)
+    def _():
+        wait_for(8, False)
+
+    spread(0)
+    put(0, classes(0, 0, early, over_end, taps_out, fir, cm, tw), False)
+
+    @pl.when(jnp.logical_not(late))
+    def _():
+        put(0, classes(1, 0, got, extra, taps_out, fir, cm, tw), True)
+        wait_for(8, False)
+
+    spread(1)
+    put(1, classes(0, 1, early, over_end, taps_out, fir, cm, tw), False)
+    whole(0, early, 15, True).wait_send()
+    whole(2, heads, 15, True).wait_send()
+    whole(1, got, 8, False).wait_recv()
+    whole(1, got, 15, True).wait_send()
 
 
 def fine_kernel(got, extra, taps, first, cm, tw, out, fir, stage, out_sem):
-    blocks = {}
-
-    def block(c, frame):
-        if (c, frame) not in blocks:
-            value = got[frame // 2, pl.ds(8 * c, 8), pl.ds(LANES * (frame % 2), LANES)]
-            if frame % 2 == 0 and frame > 0:
-                value = value + extra[frame // 2 - 1, pl.ds(8 * c, 8), :]
-            blocks[c, frame] = value
-        return blocks[c, frame]
-
-    fine_filter(1, block, lambda j: taps[1, j], fir)
-    writes = []
-    for k in range(4):
-        (re1, im1), (re3, im3) = fine_spectra(1, k, fir, cm, tw)
-        re0, im0, re2, im2 = first[k, 0, 0], first[k, 0, 1], re1, im1
-        re1, im1 = first[k, 1, 0], first[k, 1, 1]
-        sum_re, sum_im = re0 + re2, im0 + im2
-        dif_re, dif_im = re0 - re2, im0 - im2
-        odd_re, odd_im = re1 + re3, im1 + im3
-        off_re, off_im = re1 - re3, im1 - im3
-        stage[k, 0, :, 0:128] = sum_re + odd_re
-        stage[k, 1, :, 0:128] = sum_im + odd_im
-        stage[k, 0, :, 128:256] = dif_re + off_im
-        stage[k, 1, :, 128:256] = dif_im - off_re
-        stage[k, 0, :, 256:384] = sum_re - odd_re
-        stage[k, 1, :, 256:384] = sum_im - odd_im
-        stage[k, 0, :, 384:512] = dif_re - off_im
-        stage[k, 1, :, 384:512] = dif_im + off_re
-        for c in range(2):
-            write = pltpu.make_async_copy(stage.at[k, c], out.at[c, k], out_sem.at[k, c])
-            write.start()
-            writes.append(write)
-    for write in writes:
-        write.wait()
+    late = lax.axis_index("zh") == 1
+
+    def write(source, half, k):
+        rows = pl.ds(16 * half, 16)
+        return pltpu.make_async_copy(
+            source.at[:, k, rows], out.at[:, k, rows], out_sem.at[half, k]
+        )
+
+    def finish(half):
+        rows = slice(16 * half, 16 * half + 16)
+        quarters = classes(1, half, got, extra, taps, fir, cm, tw)
+        for k in range(4):
+            for d, both in enumerate(quarters):
+                lanes = slice(LANES * d, LANES * d + LANES)
+                for part, value in enumerate(both):
+                    stage[part, k, rows, lanes] = (
+                        first[part, k, rows, lanes] + value[16 * k : 16 * k + 16]
+                    )
+            write(stage, half, k).start()
+
+    @pl.when(jnp.logical_not(late))
+    def _():
+        for k in range(4):
+            write(first, 0, k).start()
+
+    @pl.when(late)
+    def _():
+        finish(0)
+
+    finish(1)
+    for half in range(2):
+        for k in range(4):
+            write(stage, half, k).wait()
 
 
 def on_device(signal, coarse_taps, fine_taps):
@@ -404,7 +464,7 @@
             jax.ShapeDtypeStruct((PEERS, 16, 256), f32),
             jax.ShapeDtypeStruct((PEERS, 16, LANES), f32),
             jax.ShapeDtypeStruct((2, FINE_TAPS, 8, LANES), f32),
-            jax.ShapeDtypeStruct((4, 2, 2, 32, LANES), f32),
+            jax.ShapeDtypeStruct((2, 4, 32, FINE), f32),
             jax.ShapeDtypeStruct((768, 256), jnp.bfloat16),
             jax.ShapeDtypeStruct((8, LANES), f32),
         ],
@@ -421,10 +481,11 @@
             pltpu.VMEM((PEERS, 1, LANES), f32),
             pltpu.VMEM((PEERS, 1, LANES), f32),
             pltpu.VMEM((2, PEERS, 16, 256), f32),
-            pltpu.VMEM((2, 256, LANES), f32),
+            pltpu.VMEM((PEERS, 16, LANES), f32),
+            pltpu.VMEM((2, LANES, LANES), f32),
             pltpu.SemaphoreType.DMA((7,)),
             pltpu.SemaphoreType.DMA((3,)),
-            pltpu.SemaphoreType.DMA((3,)),
+            pltpu.SemaphoreType.DMA((6,)),
             pltpu.SemaphoreType.REGULAR((8,)),
             pltpu.SemaphoreType.REGULAR,
         ],
@@ -439,9 +500,9 @@
         in_specs=[vmem] * 6,
         out_specs=hbm,
         scratch_shapes=[
-            pltpu.VMEM((2, 256, LANES), f32),
-            pltpu.VMEM((4, 2, 32, FINE), f32),
-            pltpu.SemaphoreType.DMA((4, 2)),
+            pltpu.VMEM((2, LANES, LANES), f32),
+            pltpu.VMEM((2, 4, 32, FINE), f32),
+            pltpu.SemaphoreType.DMA((2, 4)),
         ],
         compiler_params=pltpu.CompilerParams(vmem_limit_bytes=16 << 20),
         name="fine",

time: 23.3 us -> 22.7 us (0.974)
  the two profiles are of different devices: /device:TPU:120 before, /device:TPU:176 now
where the time goes in v5:
time: 22.7 us; the launch traced here: 22.6 us
  Pallas kernels  22.6 us (100%)
    pallas_call x1, Pallas kernels, on_device(): pl.pallas_call(gather_kernel, out_shape=[jax.ShapeDtypeStruct((PEERS, 16,...  21.2 us
    pallas_call x1, Pallas kernels, on_device(): pl.pallas_call(fine_kernel, out_shape=jax.ShapeDtypeStruct((2, 4, 32, FIN...  1.41 us

profile of v5, /device:TPU:176, one launch (start us, length us, event | category | flops | bytes accessed | tf_op | source)
XLA Modules:
  0.0 22.6 jit_solution(12300777855963780494)
XLA Ops:
  0.0 21.2 %gather.1 = (f32[16,16,256]{2,1,0:T(8,128)S(1)}, f32[16,16,128]{2,1,0:T(8,128)S(1)}, f32[2,12,8,128]{3,2,1,0:T(8,128)S(1)}, f32[2,4,32,512]{3,2,1,0:T(8,128)S(1)...) custom-call(f32[1024,128]{1,0:T(8,128)} %bitcast.5, bf16[256,512]{1,0:T(8,128)(2,1)} %constant.6.clone.m_hbm, ...), custom_call_target="tpu_custom_call" | custom-call | tf_op jit(solution)/shard_map/gather/pallas_call | solution.py:461
  21.2 1.4 %fine.1 = f32[2,4,32,512]{3,2,1,0:T(8,128)} custom-call(f32[16,16,256]{2,1,0:T(8,128)S(1)} %get-tuple-element.11.got, f32[16,16,128]{2,1,0:T(8,128)S(1)} %get-tuple-element.12.extra, f32[2,12,8,128]{3,2,1,0:T(8,128)S(1)} %get-tuple-element.13.taps, f32[2,4,32,512]{3,2,1,0:T(8,128)S(1)} %get-tuple-element.14.first, ...), custom_call_target="tpu_custom_call" | custom-call | tf_op jit(solution)/shard_map/fine/pallas_call | solution.py:497

commit v6 on v5

--- a/solution.py
+++ b/solution.py
@@ -102,10 +102,10 @@
     )
 
 
-def fine_filter(half, block, taps, fir):
+def fine_filter(start, count, block, taps, fir):
     for c in range(2):
         blocks = {}
-        for frame in range(16 * half, 16 * half + 16):
+        for frame in range(start, start + count):
             acc = None
             for j in range(min(FINE_TAPS, frame + 1)):
                 at = frame - j
@@ -113,14 +113,14 @@
                     blocks[at] = block(c, at)
                 term = taps(j) * blocks[at]
                 acc = term if acc is None else acc + term
-            fir[c, pl.ds(8 * (frame - 16 * half), 8), :] = acc
-
-
-def fine_spectra(a1, fir, cm, tw):
+            fir[c, pl.ds(8 * (frame - start), 8), :] = acc
+
+
+def fine_spectra(a1, count, fir, cm, tw):
     rows = []
     for h in range(2):
         for k in range(4):
-            parts = [fir[c, pl.ds(2 * k + h, 16, stride=8), :] for c in range(2)]
+            parts = [fir[c, pl.ds(2 * k + h, count, stride=8), :] for c in range(2)]
             rows.append(jnp.concatenate(parts, axis=1))
     high, low = split(jnp.concatenate(rows, axis=0))
     left = jnp.concatenate([high, high, low], axis=1)
@@ -128,8 +128,8 @@
     result = []
     for h in range(2):
         a = 2 * a1 + h
-        re = spectrum[64 * h : 64 * h + 64, :LANES]
-        im = spectrum[64 * h : 64 * h + 64, LANES:]
+        rows = slice(4 * count * h, 4 * count * (h + 1))
+        re, im = spectrum[rows, :LANES], spectrum[rows, LANES:]
         if a:
             cos, sin = tw[a : a + 1, :], tw[4 + a : 5 + a, :]
             re, im = re * cos + im * sin, im * cos - re * sin
@@ -146,15 +146,15 @@
     return quarters
 
 
-def classes(a1, half, blocks, over_end, taps, fir, cm, tw):
+def classes(a1, start, count, blocks, over_end, taps, fir, cm, tw):
     def block(c, frame):
         value = blocks[frame // 2, pl.ds(8 * c, 8), pl.ds(LANES * (frame % 2), LANES)]
         if frame % 2 == 0 and frame > 0:
             value = value + over_end[frame // 2 - 1, pl.ds(8 * c, 8), :]
         return value
 
-    fine_filter(half, block, lambda j: taps[a1, j], fir)
-    return fine_spectra(a1, fir, cm, tw)
+    fine_filter(start, count, block, lambda j: taps[a1, j], fir)
+    return fine_spectra(a1, count, fir, cm, tw)
 
 
 def gather_kernel(
@@ -184,8 +184,15 @@
     late = zh == 1
     patient = jnp.logical_and(zh == 0, lax.div(lax.axis_index("streams"), 4) == 1)
     turn = lax.rem(lax.div(y + 1, 2), 2)
-    odd_y = lax.rem(y, 2)
-    across = [(dy, dc) for dy in (turn, 1 - turn, 3 - odd_y, 2 + odd_y) for dc in (1, 0)]
+    def pick(*table):
+        by_y = [jnp.where(y == 2, t[2], t[3]) for t in zip(*table, strict=True)]
+        by_y = [jnp.where(y == 1, t[1], v) for t, v in zip(zip(*table), by_y, strict=True)]
+        return [jnp.where(y == 0, t[0], v) for t, v in zip(zip(*table), by_y, strict=True)]
+
+    to_early = pick((2, 1, 0, 3), (3, 0, 1, 2), (0, 1, 3, 2), (1, 0, 2, 3))
+    to_late = [turn, 1 - turn, 2 + turn, 3 - turn]
+    order = [jnp.where(late, p, q) for p, q in zip(to_early, to_late, strict=True)]
+    across = [(dy, dc) for dy in order for dc in (1, 0)]
     barrier = pltpu.get_barrier_semaphore()
     for at in across:
         pl.semaphore_signal(barrier, inc=1, device_id=named(other, *at), device_id_type=MESH)
@@ -217,11 +224,15 @@
             PEERS, 16, LANES
         )
 
-    def prepare():
+    def turned():
         loads[4].wait()
-        square = jnp.concatenate([ft[...], jnp.zeros((LANES - FINE_TAPS, FINE), jnp.float32)], axis=0)
+        square = jnp.concatenate(
+            [ft[...], jnp.zeros((LANES - FINE_TAPS, FINE), jnp.float32)], axis=0
+        )
         for k in range(4):
             ftt[pl.ds(LANES * k, LANES), :] = square[:, LANES * k : LANES * (k + 1)].T
+
+    def sorted_taps():
         by_branch = [ftt[pl.ds(a, LANES, stride=4), :].T for a in range(4)]
         odd = lax.rem(lax.broadcasted_iota(jnp.int32, (8, LANES), 0), 2) == 1
         for a1 in range(2):
@@ -322,7 +333,7 @@
         @pl.when(patient)
         def _():
             pl.semaphore_wait(barrier, 8)
-            prepare()
+            turned()
 
         for half in (slice(0, 4), slice(4, 8)):
             for at, copy in zip(across[half], zero[half], strict=True):
@@ -353,7 +364,9 @@
 
     @pl.when(jnp.logical_not(patient))
     def _():
-        prepare()
+        turned()
+
+    sorted_taps()
 
     loads[5].wait()
     loads[6].wait()
@@ -400,15 +413,15 @@
         wait_for(8, False)
 
     spread(0)
-    put(0, classes(0, 0, early, over_end, taps_out, fir, cm, tw), False)
+    put(0, classes(0, 0, 16, early, over_end, taps_out, fir, cm, tw), False)
 
     @pl.when(jnp.logical_not(late))
     def _():
-        put(0, classes(1, 0, got, extra, taps_out, fir, cm, tw), True)
+        put(0, classes(1, 0, 16, got, extra, taps_out, fir, cm, tw), True)
         wait_for(8, False)
 
     spread(1)
-    put(1, classes(0, 1, early, over_end, taps_out, fir, cm, tw), False)
+    put(1, classes(0, 16, 16, early, over_end, taps_out, fir, cm, tw), False)
     whole(0, early, 15, True).wait_send()
     whole(2, heads, 15, True).wait_send()
     whole(1, got, 8, False).wait_recv()
@@ -418,37 +431,34 @@
 def fine_kernel(got, extra, taps, first, cm, tw, out, fir, stage, out_sem):
     late = lax.axis_index("zh") == 1
 
-    def write(source, half, k):
-        rows = pl.ds(16 * half, 16)
-        return pltpu.make_async_copy(
-            source.at[:, k, rows], out.at[:, k, rows], out_sem.at[half, k]
-        )
-
-    def finish(half):
-        rows = slice(16 * half, 16 * half + 16)
-        quarters = classes(1, half, got, extra, taps, fir, cm, tw)
+    def write(source, start, count, k):
+        rows = pl.ds(start, count)
+        return pltpu.make_async_copy(source.at[:, k, rows], out.at[:, k, rows], out_sem.at[k])
+
+    def finish(start, count):
+        rows = slice(start, start + count)
+        quarters = classes(1, start, count, got, extra, taps, fir, cm, tw)
         for k in range(4):
             for d, both in enumerate(quarters):
                 lanes = slice(LANES * d, LANES * d + LANES)
                 for part, value in enumerate(both):
                     stage[part, k, rows, lanes] = (
-                        first[part, k, rows, lanes] + value[16 * k : 16 * k + 16]
+                        first[part, k, rows, lanes] + value[count * k : count * (k + 1)]
                     )
-            write(stage, half, k).start()
+            write(stage, start, count, k).start()
 
     @pl.when(jnp.logical_not(late))
     def _():
         for k in range(4):
-            write(first, 0, k).start()
+            write(first, 0, 16, k).start()
+        finish(16, 16)
 
     @pl.when(late)
     def _():
-        finish(0)
-
-    finish(1)
-    for half in range(2):
-        for k in range(4):
-            write(stage, half, k).wait()
+        finish(0, 32)
+
+    for k in range(4):
+        write(stage, 0, 32, k).wait()
 
 
 def on_device(signal, coarse_taps, fine_taps):
@@ -500,9 +510,9 @@
         in_specs=[vmem] * 6,
         out_specs=hbm,
         scratch_shapes=[
-            pltpu.VMEM((2, LANES, LANES), f32),
+            pltpu.VMEM((2, 256, LANES), f32),
             pltpu.VMEM((2, 4, 32, FINE), f32),
-            pltpu.SemaphoreType.DMA((2, 4)),
+            pltpu.SemaphoreType.DMA((4,)),
         ],
         compiler_params=pltpu.CompilerParams(vmem_limit_bytes=16 << 20),
         name="fine",

time: 22.7 us -> 22.5 us (level)
  the two profiles are of different devices: /device:TPU:176 before, /device:TPU:126 now
where the time goes in v6:
time: 22.5 us; the launch traced here: 22.3 us
  Pallas kernels  22.3 us (99%)
    pallas_call x1, Pallas kernels, on_device(): pl.pallas_call(gather_kernel, out_shape=[jax.ShapeDtypeStruct((PEERS, 16,...  21.3 us
    pallas_call x1, Pallas kernels, on_device(): pl.pallas_call(fine_kernel, out_shape=jax.ShapeDtypeStruct((2, 4, 32, FIN...  1.06 us

profile of v6, /device:TPU:126, one launch (start us, length us, event | category | flops | bytes accessed | tf_op | source)
XLA Modules:
  0.0 22.3 jit_solution(7747029834192002151)
XLA Ops:
  0.0 21.3 %gather.1 = (f32[16,16,256]{2,1,0:T(8,128)S(1)}, f32[16,16,128]{2,1,0:T(8,128)S(1)}, f32[2,12,8,128]{3,2,1,0:T(8,128)S(1)}, f32[2,4,32,512]{3,2,1,0:T(8,128)S(1)...) custom-call(f32[1024,128]{1,0:T(8,128)} %bitcast.5, bf16[256,512]{1,0:T(8,128)(2,1)} %constant.6.clone.m_hbm, ...), custom_call_target="tpu_custom_call" | custom-call | tf_op jit(solution)/shard_map/gather/pallas_call | solution.py:471
  21.3 1.1 %fine.1 = f32[2,4,32,512]{3,2,1,0:T(8,128)} custom-call(f32[16,16,256]{2,1,0:T(8,128)S(1)} %get-tuple-element.11.got, f32[16,16,128]{2,1,0:T(8,128)S(1)} %get-tuple-element.12.extra, f32[2,12,8,128]{3,2,1,0:T(8,128)S(1)} %get-tuple-element.13.taps, f32[2,4,32,512]{3,2,1,0:T(8,128)S(1)} %get-tuple-element.14.first, ...), custom_call_target="tpu_custom_call" | custom-call | tf_op jit(solution)/shard_map/fine/pallas_call | solution.py:507

commit v7 on v6

--- a/solution.py
+++ b/solution.py
@@ -19,7 +19,7 @@
 PEERS = 16
 LANES = 128
 HEAD = 16
-TAIL = 32
+TAIL = 40
 ROWS = 1024
 HALF = 512
 MESH = pl.DeviceIdType.MESH
@@ -371,10 +371,6 @@
     loads[5].wait()
     loads[6].wait()
 
-    def wait_for(count, near):
-        whole(0, early, count, near).wait_recv()
-        whole(2, heads, count, near).wait_recv()
-
     row = lax.rem(lax.broadcasted_iota(jnp.int32, (256, 256), 0), 8)
     column = lax.broadcasted_iota(jnp.int32, (256, 256), 1)
     lane = lax.rem(column, LANES)
@@ -405,12 +401,15 @@
                     value = value + first[part, :, rows, lanes]
                 first[part, :, rows, lanes] = value
 
-    wait_for(7, True)
+    whole(0, early, 7, True).wait_recv()
     whole(1, got, 7, True).wait_recv()
+    whole(2, heads, 7, True).wait_recv()
 
     @pl.when(late)
     def _():
-        wait_for(8, False)
+        whole(2, heads, 8, False).wait_recv()
+        spread(1)
+        whole(0, early, 8, False).wait_recv()
 
     spread(0)
     put(0, classes(0, 0, 16, early, over_end, taps_out, fir, cm, tw), False)
@@ -418,9 +417,10 @@
     @pl.when(jnp.logical_not(late))
     def _():
         put(0, classes(1, 0, 16, got, extra, taps_out, fir, cm, tw), True)
-        wait_for(8, False)
-
-    spread(1)
+        whole(2, heads, 8, False).wait_recv()
+        spread(1)
+        whole(0, early, 8, False).wait_recv()
+
     put(1, classes(0, 16, 16, early, over_end, taps_out, fir, cm, tw), False)
     whole(0, early, 15, True).wait_send()
     whole(2, heads, 15, True).wait_send()

time: 22.5 us -> 22.4 us (level)
  the two profiles are of different devices: /device:TPU:126 before, /device:TPU:32 now
where the time goes in v7:
time: 22.4 us; the launch traced here: 22.3 us
  Pallas kernels  22.3 us (100%)
    pallas_call x1, Pallas kernels, on_device(): pl.pallas_call(gather_kernel, out_shape=[jax.ShapeDtypeStruct((PEERS, 16,...  21.2 us
    pallas_call x1, Pallas kernels, on_device(): pl.pallas_call(fine_kernel, out_shape=jax.ShapeDtypeStruct((2, 4, 32, FIN...  1.06 us

profile of v7, /device:TPU:32, one launch (start us, length us, event | category | flops | bytes accessed | tf_op | source)
XLA Modules:
  0.0 22.3 jit_solution(4654722369999393436)
XLA Ops:
  0.0 21.2 %gather.1 = (f32[16,16,256]{2,1,0:T(8,128)S(1)}, f32[16,16,128]{2,1,0:T(8,128)S(1)}, f32[2,12,8,128]{3,2,1,0:T(8,128)S(1)}, f32[2,4,32,512]{3,2,1,0:T(8,128)S(1)...) custom-call(f32[1024,128]{1,0:T(8,128)} %bitcast.5, bf16[256,512]{1,0:T(8,128)(2,1)} %constant.6.clone.m_hbm, ...), custom_call_target="tpu_custom_call" | custom-call | tf_op jit(solution)/shard_map/gather/pallas_call | solution.py:471
  21.2 1.1 %fine.1 = f32[2,4,32,512]{3,2,1,0:T(8,128)} custom-call(f32[16,16,256]{2,1,0:T(8,128)S(1)} %get-tuple-element.11.got, f32[16,16,128]{2,1,0:T(8,128)S(1)} %get-tuple-element.12.extra, f32[2,12,8,128]{3,2,1,0:T(8,128)S(1)} %get-tuple-element.13.taps, f32[2,4,32,512]{3,2,1,0:T(8,128)S(1)} %get-tuple-element.14.first, ...), custom_call_target="tpu_custom_call" | custom-call | tf_op jit(solution)/shard_map/fine/pallas_call | solution.py:507

commit v8 on v7

--- a/solution.py
+++ b/solution.py
@@ -175,8 +175,8 @@
         pltpu.make_async_copy(c_hbm, cm, load_sem.at[5]),
         pltpu.make_async_copy(t_hbm, tw, load_sem.at[6]),
     ]
-    for load in loads[:4]:
-        load.start()
+    for k in (1, 0, 3, 2):
+        loads[k].start()
     zh, y, c = (lax.axis_index(axis) for axis in TM)
     mine = flat(zh, y, c)
     own = 2 * y + c
@@ -189,7 +189,7 @@
         by_y = [jnp.where(y == 1, t[1], v) for t, v in zip(zip(*table), by_y, strict=True)]
         return [jnp.where(y == 0, t[0], v) for t, v in zip(zip(*table), by_y, strict=True)]
 
-    to_early = pick((2, 1, 0, 3), (3, 0, 1, 2), (0, 1, 3, 2), (1, 0, 2, 3))
+    to_early = pick((2, 1, 0, 3), (3, 0, 1, 2), (1, 0, 3, 2), (0, 1, 2, 3))
     to_late = [turn, 1 - turn, 2 + turn, 3 - turn]
     order = [jnp.where(late, p, q) for p, q in zip(to_early, to_late, strict=True)]
     across = [(dy, dc) for dy in order for dc in (1, 0)]

time: 22.4 us -> 22.4 us (level)
  no operation moved by 1% of the time
where the time goes in v8:
time: 22.4 us; the launch traced here: 22.3 us
  Pallas kernels  22.3 us (100%)
    pallas_call x1, Pallas kernels, on_device(): pl.pallas_call(gather_kernel, out_shape=[jax.ShapeDtypeStruct((PEERS, 16,...  21.2 us
    pallas_call x1, Pallas kernels, on_device(): pl.pallas_call(fine_kernel, out_shape=jax.ShapeDtypeStruct((2, 4, 32, FIN...  1.06 us

profile of v8, /device:TPU:32, one launch (start us, length us, event | category | flops | bytes accessed | tf_op | source)
XLA Modules:
  0.0 22.3 jit_solution(11767787766070733149)
XLA Ops:
  0.0 21.2 %gather.1 = (f32[16,16,256]{2,1,0:T(8,128)S(1)}, f32[16,16,128]{2,1,0:T(8,128)S(1)}, f32[2,12,8,128]{3,2,1,0:T(8,128)S(1)}, f32[2,4,32,512]{3,2,1,0:T(8,128)S(1)...) custom-call(f32[1024,128]{1,0:T(8,128)} %bitcast.5, bf16[256,512]{1,0:T(8,128)(2,1)} %constant.6.clone.m_hbm, ...), custom_call_target="tpu_custom_call" | custom-call | tf_op jit(solution)/shard_map/gather/pallas_call | solution.py:471
  21.2 1.1 %fine.1 = f32[2,4,32,512]{3,2,1,0:T(8,128)} custom-call(f32[16,16,256]{2,1,0:T(8,128)S(1)} %get-tuple-element.11.got, f32[16,16,128]{2,1,0:T(8,128)S(1)} %get-tuple-element.12.extra, f32[2,12,8,128]{3,2,1,0:T(8,128)S(1)} %get-tuple-element.13.taps, f32[2,4,32,512]{3,2,1,0:T(8,128)S(1)} %get-tuple-element.14.first, ...), custom_call_target="tpu_custom_call" | custom-call | tf_op jit(solution)/shard_map/fine/pallas_call | solution.py:507

commit v9 on v7

--- a/solution.py
+++ b/solution.py
@@ -326,7 +326,7 @@
         picked = jnp.where(chosen, result[16 * d : 16 * d + 16], 0.0)
         tails[d] = jnp.sum(picked, axis=0, keepdims=True)
     heads[mine] = tails[mine]
-    start([*two, *zero[4:], *one[4:]])
+    start([*zero[4:], *two, *one[4:]])
 
     @pl.when(jnp.logical_not(late))
     def _():

time: 22.4 us -> 23.1 us (1.031)
  the two profiles are of different devices: /device:TPU:32 before, /device:TPU:64 now
where the time goes in v9:
time: 23.1 us; the launch traced here: 23 us
  Pallas kernels  23 us (100%)
    pallas_call x1, Pallas kernels, on_device(): pl.pallas_call(gather_kernel, out_shape=[jax.ShapeDtypeStruct((PEERS, 16,...  21.9 us
    pallas_call x1, Pallas kernels, on_device(): pl.pallas_call(fine_kernel, out_shape=jax.ShapeDtypeStruct((2, 4, 32, FIN...  1.06 us

profile of v9, /device:TPU:64, one launch (start us, length us, event | category | flops | bytes accessed | tf_op | source)
XLA Modules:
  0.0 23.0 jit_solution(18112119626751200298)
XLA Ops:
  0.0 21.9 %gather.1 = (f32[16,16,256]{2,1,0:T(8,128)S(1)}, f32[16,16,128]{2,1,0:T(8,128)S(1)}, f32[2,12,8,128]{3,2,1,0:T(8,128)S(1)}, f32[2,4,32,512]{3,2,1,0:T(8,128)S(1)...) custom-call(f32[1024,128]{1,0:T(8,128)} %bitcast.5, bf16[256,512]{1,0:T(8,128)(2,1)} %constant.6.clone.m_hbm, ...), custom_call_target="tpu_custom_call" | custom-call | tf_op jit(solution)/shard_map/gather/pallas_call | solution.py:471
  21.9 1.1 %fine.1 = f32[2,4,32,512]{3,2,1,0:T(8,128)} custom-call(f32[16,16,256]{2,1,0:T(8,128)S(1)} %get-tuple-element.11.got, f32[16,16,128]{2,1,0:T(8,128)S(1)} %get-tuple-element.12.extra, f32[2,12,8,128]{3,2,1,0:T(8,128)S(1)} %get-tuple-element.13.taps, f32[2,4,32,512]{3,2,1,0:T(8,128)S(1)} %get-tuple-element.14.first, ...), custom_call_target="tpu_custom_call" | custom-call | tf_op jit(solution)/shard_map/fine/pallas_call | solution.py:507
